TPU v7x, 16 devices: a whole 2x2x2 slice. The times are simulated.
16 devices in a mesh: rep: 1, dp: 16 (over x, y, z, core).
Axes of the slice: x: 2, y: 2, z: 2, core: 2. Of those that a mesh axis runs over, the one named last changes fastest.
Arguments:
- g_w_gate: bfloat16 [16, 2, 1024, 2816], P(('rep', 'dp'))
- g_w_up: bfloat16 [16, 2, 1024, 2816], P(('rep', 'dp'))
- g_w_down: bfloat16 [16, 2, 2816, 1024], P(('rep', 'dp'))
- w_gate: bfloat16 [2, 1024, 2816], replicated
- w_up: bfloat16 [2, 1024, 2816], replicated
- w_down: bfloat16 [2, 2816, 1024], replicated
- m_w_gate: float32 [2, 1024, 2816], P(None, 'dp')
- m_w_up: float32 [2, 1024, 2816], P(None, 'dp')
- m_w_down: float32 [2, 2816, 1024], P(None, 'dp')
- v_w_gate: float32 [2, 1024, 2816], P(None, 'dp')
- v_w_up: float32 [2, 1024, 2816], P(None, 'dp')
- v_w_down: float32 [2, 2816, 1024], P(None, 'dp')
Outputs:
- output 1: bfloat16 [2, 1024, 2816], P('rep')
- output 2: bfloat16 [2, 1024, 2816], P('rep')
- output 3: bfloat16 [2, 2816, 1024], P('rep')
- output 4: float32 [2, 1024, 2816], P('rep', 'dp')
- output 5: float32 [2, 1024, 2816], P('rep', 'dp')
- output 6: float32 [2, 2816, 1024], P('rep', 'dp')
- output 7: float32 [2, 1024, 2816], P('rep', 'dp')
- output 8: float32 [2, 1024, 2816], P('rep', 'dp')
- output 9: float32 [2, 2816, 1024], P('rep', 'dp')
All inputs are finite; a program needn't handle non-finite values.
Results may differ from a plain program's by a relative error of at most 0.022.
Values are sent between devices in bfloat16 or wider.
A program may use at most 2 GiB of HBM per device.

v0:
```python
import jax
import jax.numpy as jnp
from jax import lax
from jax.sharding import PartitionSpec as P


def adamw(w, m, v, g):
    m = 0.9 * m + 0.1 * g
    v = 0.95 * v + 0.05 * g * g
    step = m * lax.rsqrt(v + 1e-8) + 0.1 * w
    return (w - 0.02 * step).astype(jnp.bfloat16), m, v


def solution(mesh):
    def step(*arrays):
        terms, weights, m, v = (arrays[i : i + 3] for i in (0, 3, 6, 9))
        gradients = [lax.psum_scatter(t[0], "dp", scatter_dimension=1, tiled=True).astype(jnp.float32) for t in terms]
        me = lax.axis_index("dp")
        own = [lax.dynamic_slice_in_dim(w, me * one.shape[1], one.shape[1], 1).astype(jnp.float32) for w, one in zip(weights, m, strict=True)]
        new = [adamw(w, m, v, g) for w, m, v, g in zip(own, m, v, gradients, strict=True)]
        whole = [lax.all_gather(one[0], "dp", axis=1, tiled=True) for one in new]
        return (*whole, *(one[1] for one in new), *(one[2] for one in new))

    all_of, cut = P(None, None, None), P(None, "dp", None)
    return jax.shard_map(
        step,
        mesh=mesh,
        in_specs=(P(("rep", "dp"), None, None, None),) * 3 + (all_of,) * 3 + (cut,) * 6,
        out_specs=(P("rep", None, None),) * 3 + (P("rep", "dp", None),) * 6,
        check_vma=False,
    )
```

profile of v0, /device:TPU:0, one launch (start us, length us, event | category | flops | bytes accessed | tf_op | source)
XLA Modules:
  0.0 606.7 jit_solution(16022322014245889233)
XLA Ops:
  7.2 0.0 reduce-scatter.8.cloned.1.call-start
  7.2 0.7 reduce-scatter.8.cloned.1.call-update
  7.9 0.0 reduce-scatter.6.cloned.1.call-start
  8.0 0.7 reduce-scatter.6.cloned.1.call-update
  8.7 0.0 reduce-scatter.4.cloned.1.call-start
  8.7 0.0 copy-start.1
  8.7 0.0 copy-start.2
  8.7 0.7 reduce-scatter.4.cloned.1.call-update
  9.4 0.0 all-gather.8.cloned.1.call-start
  9.4 124.5 %reduce-scatter.8.cloned.1.call-done = bf16[2,176,1024]{2,1,0:T(8,128)(2,1)} async-done(((bf16[2,2816,1024]{2,1,0:T(8,128)(2,1)}), bf16[2,176,1024]{2,1,0:T(8,128)(2,1)}) %reduce-scatter.8.cloned.1.call-update) | async-done | bytes 720912 | tf_op jit(solution)/shard_map/reduce_scatter | solution.py:17
  133.9 0.0 copy-done.1
  133.9 0.0 copy-done.2
  133.9 3.6 fusion.10
  137.5 0.0 all-gather.8.cloned.1.call-update
  137.5 0.0 all-gather.6.cloned.1.call-start
  137.6 123.0 %reduce-scatter.6.cloned.1.call-done = bf16[2,64,2816]{2,1,0:T(8,128)(2,1)} async-done(((bf16[2,1024,2816]{2,1,0:T(8,128)(2,1)}), bf16[2,64,2816]{2,1,0:T(8,128)(2,1)}) %reduce-scatter.6.cloned.1.call-update) | async-done | bytes 720912 | tf_op jit(solution)/shard_map/reduce_scatter | solution.py:17
  260.5 0.0 copy-start.3
  260.5 0.0 copy-start.4
  260.5 4.5 fusion.6
  265.1 0.0 all-gather.6.cloned.1.call-update
  265.1 0.0 all-gather.4.cloned.1.call-start
  265.1 122.0 %reduce-scatter.4.cloned.1.call-done = bf16[2,64,2816]{2,1,0:T(8,128)(2,1)} async-done(((bf16[2,1024,2816]{2,1,0:T(8,128)(2,1)}), bf16[2,64,2816]{2,1,0:T(8,128)(2,1)}) %reduce-scatter.4.cloned.1.call-update) | async-done | bytes 720912 | tf_op jit(solution)/shard_map/reduce_scatter | solution.py:17
  387.1 0.0 copy-done.3
  387.1 0.0 copy-done.4
  387.1 3.5 fusion.2
  390.6 0.0 all-gather.4.cloned.1.call-update
  390.6 61.8 %all-gather.8.cloned.1.call-done = bf16[2,2816,1024]{2,1,0:T(8,128)(2,1)} async-done(((bf16[2,176,1024]{2,1,0:T(8,128)(2,1)}), bf16[2,2816,1024]{2,1,0:T(8,128)(2,1)}) %all-gather.8.cloned.1.call-update) | async-done | bytes 11534352 | tf_op jit(solution)/shard_map/all_gather | solution.py:21
  452.4 61.7 %all-gather.6.cloned.1.call-done = bf16[2,1024,2816]{2,1,0:T(8,128)(2,1)} async-done(((bf16[2,64,2816]{2,1,0:T(8,128)(2,1)}), bf16[2,1024,2816]{2,1,0:T(8,128)(2,1)}) %all-gather.6.cloned.1.call-update) | async-done | bytes 11534352 | tf_op jit(solution)/shard_map/all_gather | solution.py:21
  514.1 61.8 %all-gather.4.cloned.1.call-done = bf16[2,1024,2816]{2,1,0:T(8,128)(2,1)} async-done(((bf16[2,64,2816]{2,1,0:T(8,128)(2,1)}), bf16[2,1024,2816]{2,1,0:T(8,128)(2,1)}) %all-gather.4.cloned.1.call-update) | async-done | bytes 11534352 | tf_op jit(solution)/shard_map/all_gather | solution.py:21
  575.9 0.0 copy-start
  575.9 0.0 slice-start
  575.9 0.0 slice-start.1
  575.9 11.7 %copy.24 = bf16[2,1024,2816]{2,1,0:T(8,128)(2,1)} copy(bf16[2,1024,2816]{2,1,0:T(8,128)(2,1)} %all-gather.4.cloned.1.call-done) | data formatting | bytes 23068672
  587.6 0.0 copy-done
  587.6 0.0 slice-start.2
  587.6 5.8 copy.25
  593.4 0.0 slice-done
  593.4 0.8 slice-done.1
  594.2 1.2 slice-done.2
  595.4 4.4 copy.26
  (1 shorter events, 0.0 us)
Async XLA Ops:
  7.2 126.7 %reduce-scatter.8.cloned.1.call-start = ((), (), s32[]{:S(2)}) async-start(), calls=%async_computation.7 | async-start | bytes 12255232 | tf_op jit(solution)/shard_map/reduce_scatter | solution.py:17
  7.9 252.6 %reduce-scatter.6.cloned.1.call-start = ((), (), s32[]{:S(2)}) async-start(), calls=%async_computation.5 | async-start | bytes 12255232 | tf_op jit(solution)/shard_map/reduce_scatter | solution.py:17
  8.7 378.5 %reduce-scatter.4.cloned.1.call-start = ((), (), s32[]{:S(2)}) async-start(), calls=%async_computation.3 | async-start | bytes 12255232 | tf_op jit(solution)/shard_map/reduce_scatter | solution.py:17
  8.7 125.2 %copy-start.1 = (f32[2,176,1024]{2,1,0:T(8,128)S(1)}, f32[2,176,1024]{2,1,0:T(8,128)}, u32[]{:S(2)}) copy-start(f32[2,176,1024]{2,1,0:T(8,128)} %param.23) | copy-start | bytes 4325380
  8.7 125.2 %copy-start.2 = (f32[2,176,1024]{2,1,0:T(8,128)S(1)}, f32[2,176,1024]{2,1,0:T(8,128)}, u32[]{:S(2)}) copy-start(f32[2,176,1024]{2,1,0:T(8,128)} %param.20) | copy-start | bytes 4325380
  9.4 443.0 %all-gather.8.cloned.1.call-start = ((), (), s32[]{:S(2)}) async-start(), calls=%async_computation.8 | async-start | bytes 12255232 | tf_op jit(solution)/shard_map/all_gather | solution.py:21
  137.5 376.6 %all-gather.6.cloned.1.call-start = ((), (), s32[]{:S(2)}) async-start(), calls=%async_computation.6 | async-start | bytes 12255232 | tf_op jit(solution)/shard_map/all_gather | solution.py:21
  260.5 126.6 %copy-start.3 = (f32[2,64,2816]{2,1,0:T(8,128)S(1)}, f32[2,64,2816]{2,1,0:T(8,128)}, u32[]{:S(2)}) copy-start(f32[2,64,2816]{2,1,0:T(8,128)} %param.21) | copy-start | bytes 4325380
  260.5 126.6 %copy-start.4 = (f32[2,64,2816]{2,1,0:T(8,128)S(1)}, f32[2,64,2816]{2,1,0:T(8,128)}, u32[]{:S(2)}) copy-start(f32[2,64,2816]{2,1,0:T(8,128)} %param.18) | copy-start | bytes 4325380
  265.1 310.8 %all-gather.4.cloned.1.call-start = ((), (), s32[]{:S(2)}) async-start(), calls=%async_computation.4 | async-start | bytes 12255232 | tf_op jit(solution)/shard_map/all_gather | solution.py:21
  575.9 11.7 %copy-start = (bf16[2,1024,2816]{2,1,0:T(8,128)(2,1)S(1)}, bf16[2,1024,2816]{2,1,0:T(8,128)(2,1)}, u32[]{:S(2)}) copy-start(bf16[2,1024,2816]{2,1,0:T(8,128)(2,1)} %all-gather.6.cloned.1.call-done) | copy-start | bytes 34603012
  575.9 17.5 %slice-start = ((s8[11534336]{0:T(1024)(128)(4,1)}), s8[4194304]{0:T(1024)(128)(4,1)S(1)}, s32[]{:S(2)}) async-start(s8[11534336]{0:T(1024)(128)(4,1)} %bitcast.6), calls=%async_computation.9 | async-start | bytes 8388608
  575.9 18.3 %slice-start.1 = ((s8[11534336]{0:T(1024)(128)(4,1)}), s8[4194304]{0:T(1024)(128)(4,1)S(1)}, s32[]{:S(2)}) async-start(s8[11534336]{0:T(1024)(128)(4,1)} %bitcast.6), calls=%async_computation.10 | async-start | bytes 8388608
  587.6 7.9 %slice-start.2 = ((s8[11534336]{0:T(1024)(128)(4,1)}), s8[3145728]{0:T(1024)(128)(4,1)S(1)}, s32[]{:S(2)}) async-start(s8[11534336]{0:T(1024)(128)(4,1)} %bitcast.6), calls=%async_computation.11 | async-start | bytes 6291456
Sparse Core Ops, SparseCore 0:
  10.3 123.6 reduce-scatter.7
  136.2 124.2 reduce-scatter.5
  262.8 124.2 reduce-scatter.3
  389.8 62.5 all-gather.7
  455.1 59.0 all-gather.5
  516.8 59.0 all-gather.3
where the time goes:
time: 607 us
  waiting for transfers between devices  557 us (92%)
  local copies, waits for them, and re-layouts  24 us (4%)
  between operations  14.2 us (2%)
  other arithmetic  11.6 us (2%)
    reduce_scatter x3, waiting for transfers between devices, step(): lax.psum_scatter(t[0], 'dp', scatter_dimension=1, tiled=True)  369 us
    all_gather x3, waiting for transfers between devices, step(): whole = [lax.all_gather(one[0], 'dp', axis=1, tiled=True) for one in new]  185 us
    unnamed x19, local copies, waits for them, and re-layouts  24 us
  transfers between devices with their start and end apart: 6, of which 6 were waited for; matrix products, arithmetic and copies ran while one was open for 2% of the time, Pallas kernels for 0%

commit v1 on v0

v1 whole, which is shorter than its diff:
```python
import jax
import jax.numpy as jnp
from jax import lax
from jax.experimental import pallas as pl
from jax.experimental.pallas import tpu as pltpu
from jax.sharding import PartitionSpec as P

BF16, F32 = jnp.bfloat16, jnp.float32
MESH = pl.DeviceIdType.MESH
LAYERS = 2
ORDERS = ((0, 1, 2), (1, 2, 0), (2, 0, 1))
STRIDES = (8, 4, 2)
SLAB = 16


def adamw(w, m, v, g):
    m = 0.9 * m + 0.1 * g
    v = 0.95 * v + 0.05 * g * g
    step = m * lax.rsqrt(v + 1e-8) + 0.1 * w
    return (w - 0.02 * step).astype(BF16), m, v


class Weight:
    def __init__(self, order, where, core, **refs):
        self.order, self.core = order, core
        self.mine = [where[axis] for axis in order]
        self.__dict__.update(refs)

    def place(self, *stages):
        xyz = [None] * 3
        for axis, coordinate in zip(self.order, stages, strict=True):
            xyz[axis] = coordinate
        return tuple(xyz)

    def block(self, keep1, keep2, keep3):
        return self.place(*(1 - m + k * (2 * m - 1) for m, k in zip(self.mine, (keep1, keep2, keep3), strict=True)))


def kernel(*refs):
    g_refs, w_refs, m_refs, v_refs = (refs[i : i + 3] for i in (0, 3, 6, 9))
    all_refs, m_outs, v_outs = (refs[i : i + 3] for i in (12, 15, 18))
    firsts, seconds, thirds, olds = (refs[i : i + 3] for i in (21, 24, 27, 30))
    load_sem, rest_sem, mv_sem, pair_sem, s1_sem, s2_sem, s3_sem, a3_sem, a2_sem, a1_sem, a0_sem, send_sem, third_sem, free_sem, read_sem = refs[33:]

    me = lax.axis_index("dp")
    core = me % 2
    where = [(me // s) % 2 for s in STRIDES]
    partners = [me + s * (1 - 2 * b) for s, b in zip(STRIDES, where, strict=True)]
    pair = me + 1 - 2 * core

    weights = [
        Weight(
            ORDERS[i], where, core, i=i, g=g_refs[i], all=all_refs[i], m=m_outs[i], v=v_outs[i],
            first=firsts[i], second=seconds[i], third=thirds[i], old=olds[i],
            to=[partners[axis] for axis in ORDERS[i]],
        )
        for i in range(3)
    ]

    def remote(src, dst, send, recv, device):
        return pltpu.make_async_remote_copy(
            src_ref=src, dst_ref=dst, send_sem=send, recv_sem=recv, device_id={"dp": device}, device_id_type=MESH
        )

    def unit(w, keep1, k):
        return (k % 2, *w.block(keep1, k // 4, (k // 2) % 2))

    def load(w, k):
        at = (*unit(w, 0, k), core)
        return pltpu.make_async_copy(w.g.at[at], w.all.at[at], load_sem.at[w.i, k])

    def load_rest(w):
        at = (slice(None), *w.place(w.mine[0], slice(None), slice(None)), core)
        return pltpu.make_async_copy(w.g.at[at], w.all.at[at], rest_sem.at[w.i])

    def own_block(w):
        return (slice(None), *w.block(1, 1, 1), core)

    def moments(w):
        i = w.i
        return (
            pltpu.make_async_copy(m_refs[i], w.m, mv_sem.at[i, 0]),
            pltpu.make_async_copy(v_refs[i], w.v, mv_sem.at[i, 1]),
            pltpu.make_async_copy(w_refs[i].at[own_block(w)], w.old, mv_sem.at[i, 2]),
        )

    def to_pair(w, keep1, k):
        at = unit(w, keep1, k)
        return remote(w.g.at[(*at, 1 - core)], w.all.at[(*at, core)], send_sem.at[w.i, 0], pair_sem.at[w.i, 8 * keep1 + k], pair)

    def first(w, k):
        at = unit(w, 0, k)
        return remote(w.all.at[(*at, core)], w.first.at[k], send_sem.at[w.i, 1], s1_sem.at[w.i, k], w.to[0])

    def second(w, k):
        at = (k % 2, *w.block(1, 0, k // 2))
        return remote(w.all.at[(*at, core)], w.second.at[k], send_sem.at[w.i, 2], s2_sem.at[w.i, k], w.to[1])

    def third(w, k):
        at = (k, *w.block(1, 1, 0))
        return remote(w.all.at[(*at, core)], w.third.at[k], third_sem.at[w.i, k], s3_sem.at[w.i, k], w.to[2])

    def tell(w, stage):
        pl.semaphore_signal(free_sem.at[w.i, stage], inc=1, device_id={"dp": w.to[stage]}, device_id_type=MESH)

    def told(w, stage):
        pl.semaphore_wait(free_sem.at[w.i, stage], 1)

    def gather3(w, k):
        at = (k, *w.block(1, 1, 1), core)
        return remote(w.all.at[at], w.all.at[at], send_sem.at[w.i, 4], a3_sem.at[w.i, k], w.to[2])

    def gather2(w, k):
        at = (k % 2, *w.block(1, 1, 1 - k // 2), core)
        return remote(w.all.at[at], w.all.at[at], send_sem.at[w.i, 5], a2_sem.at[w.i, k], w.to[1])

    def gather1(w, k):
        at = (k % 2, *w.block(1, 1 - k // 4, 1 - (k // 2) % 2), core)
        return remote(w.all.at[at], w.all.at[at], send_sem.at[w.i, 6], a1_sem.at[w.i, k], w.to[0])

    def gather0(w, keep1, k):
        at = (k % 2, *w.block(keep1, 1 - k // 4, 1 - (k // 2) % 2), core)
        return remote(w.all.at[at], w.all.at[at], send_sem.at[w.i, 7], a0_sem.at[w.i], pair)

    def total(w, at, rows, *others):
        sum_ = w.all[(*at, core, rows, slice(None))].astype(F32) + w.all[(*at, 1 - core, rows, slice(None))].astype(F32)
        for other, k in others:
            sum_ = sum_ + other[k, rows, :].astype(F32)
        return sum_

    def add(w, at, *others):
        @pl.loop(0, w.old.shape[1] // SLAB)
        def _(r):
            rows = pl.ds(pl.multiple_of(r * SLAB, SLAB), SLAB)
            w.all[(*at, core, rows, slice(None))] = total(w, at, rows, *others).astype(BF16)

    def each(n, body):
        @pl.loop(0, n)
        def _(k):
            body(k)

    def start_loads(k):
        for w in weights:
            load(w, k).start()

    each(8, start_loads)

    barrier = pltpu.get_barrier_semaphore()
    for device in (pair, *partners):
        pl.semaphore_signal(barrier, inc=1, device_id={"dp": device}, device_id_type=MESH)
    pl.semaphore_wait(barrier, 4)

    for keep1 in (0, 1):

        def start_pair(k, keep1=keep1):
            for w in weights:
                to_pair(w, keep1, k).start()

        each(8, start_pair)
    for w in weights:
        load_rest(w).start()
    for w in weights:
        for copy in moments(w):
            copy.start()

    def stage1(k):
        for w in weights:
            load(w, k).wait()
            to_pair(w, 0, k).wait_recv()
            add(w, unit(w, 0, k))
        for w in weights:
            first(w, k).start()

    each(8, stage1)
    for w in weights:
        load_rest(w).wait()

    def stage2(k):
        for w in weights:
            to_pair(w, 1, k).wait_recv()
            first(w, k).wait_recv()
            add(w, unit(w, 1, k), (w.first, k))
        for w in weights:
            second(w, k).start()

    each(4, stage2)

    def stage3(k):
        for w in weights:
            to_pair(w, 1, 4 + k).wait_recv()
            first(w, 4 + k).wait_recv()
            second(w, k).wait_recv()
            add(w, unit(w, 1, 4 + k), (w.first, 4 + k), (w.second, k))
        for w in weights:
            third(w, k).start()

    each(2, stage3)
    for w in weights:
        for copy in moments(w):
            copy.wait()
        remote(w.first, w.first, send_sem.at[w.i, 1], s1_sem.at[w.i, 0], pair).wait_send()
        tell(w, 0)
        remote(w.second, w.second, send_sem.at[w.i, 2], s2_sem.at[w.i, 0], pair).wait_send()
        tell(w, 1)

    def update(k):
        for w in weights:
            to_pair(w, 1, 6 + k).wait_recv()
            first(w, 6 + k).wait_recv()
            second(w, 2 + k).wait_recv()
            third(w, k).wait()
            tell(w, 2)
            at = (k, *w.block(1, 1, 1))

            @pl.loop(0, w.old.shape[1] // SLAB)
            def _(r, w=w, at=at):
                rows = pl.ds(pl.multiple_of(r * SLAB, SLAB), SLAB)
                g = total(w, at, rows, (w.first, 6 + k), (w.second, 2 + k), (w.third, k)).astype(BF16).astype(F32)
                new, m, v = adamw(w.old[k, rows, :].astype(F32), w.m[k, rows, :], w.v[k, rows, :], g)
                w.m[k, rows, :] = m
                w.v[k, rows, :] = v
                w.all[(*at, core, rows, slice(None))] = new

        for w in weights:
            told(w, 2)
            gather3(w, k).start()

    each(2, update)

    def own21(k):
        for w in weights:
            gather2(w, k).start()
        for w in weights:
            gather1(w, k).start()

    for w in weights:
        told(w, 1)
        told(w, 0)
    each(2, own21)

    pl.semaphore_signal(read_sem, inc=1, device_id={"dp": pair}, device_id_type=MESH)
    pl.semaphore_wait(read_sem, 1)

    def own(k):
        for w in weights:
            gather0(w, 1, k).start()

    each(2, own)

    def back3(k):
        for w in weights:
            gather3(w, k).wait_recv()
            gather2(w, 2 + k).start()
        for w in weights:
            gather1(w, 2 + k).start()
            gather0(w, 1, 2 + k).start()

    each(2, back3)

    def back2(k):
        for w in weights:
            gather2(w, k).wait_recv()
            gather1(w, 4 + k).start()
            gather0(w, 1, 4 + k).start()

    each(4, back2)

    def back1(k):
        for w in weights:
            gather1(w, k).wait_recv()
            gather0(w, 0, k).start()

    each(8, back1)

    for w in weights:
        theirs = w.all.at[:, :, :, :, 1 - core]
        remote(theirs, theirs, send_sem.at[w.i, 7], a0_sem.at[w.i], pair).wait_recv()
    for w in weights:
        mine = w.all.at[:, :, :, :, core]
        for n, ref in ((0, mine), (4, w.third), (5, w.second), (6, w.first), (7, mine)):
            remote(ref, ref, send_sem.at[w.i, n], a0_sem.at[w.i], pair).wait_send()


def put(*refs):
    sem = refs[-1]
    copies = [
        pltpu.make_async_copy(refs[i].at[k], refs[9 + i].at[k], sem.at[i, k]) for i in range(9) for k in range(LAYERS)
    ]
    for copy in copies:
        copy.start()
    for copy in copies:
        copy.wait()


def solution(mesh):
    def step(*arrays):
        shapes = [a.shape[1:] for a in arrays[6:9]]

        def cut(a, i):
            return a.reshape(LAYERS, 2, 2, 2, 2, *shapes[i])

        operands = [cut(a, n % 3) for n, a in enumerate(arrays[:6])] + list(arrays[6:])
        blocks = [(n, rows, columns) for n in (8, 4, 2, LAYERS) for rows, columns in shapes]
        outs = pl.pallas_call(
            kernel,
            out_shape=[pltpu.VMEM((LAYERS, 2, 2, 2, 2, *s), BF16) for s in shapes] + [pltpu.VMEM((LAYERS, *s), F32) for s in shapes] * 2,
            in_specs=[pl.BlockSpec(memory_space=pl.ANY)] * 12,
            out_specs=[pl.BlockSpec(memory_space=pltpu.VMEM)] * 9,
            scratch_shapes=[
                *(pltpu.VMEM(s, BF16) for s in blocks),
                pltpu.SemaphoreType.DMA((3, 8)),
                pltpu.SemaphoreType.DMA((3,)),
                pltpu.SemaphoreType.DMA((3, 3)),
                pltpu.SemaphoreType.DMA((3, 16)),
                pltpu.SemaphoreType.DMA((3, 8)),
                pltpu.SemaphoreType.DMA((3, 4)),
                pltpu.SemaphoreType.DMA((3, 2)),
                pltpu.SemaphoreType.DMA((3, 2)),
                pltpu.SemaphoreType.DMA((3, 4)),
                pltpu.SemaphoreType.DMA((3, 8)),
                pltpu.SemaphoreType.DMA((3,)),
                pltpu.SemaphoreType.DMA((3, 8)),
                pltpu.SemaphoreType.DMA((3, 2)),
                pltpu.SemaphoreType.REGULAR((3, 3)),
                pltpu.SemaphoreType.REGULAR,
            ],
            compiler_params=pltpu.CompilerParams(collective_id=0, has_side_effects=True, vmem_limit_bytes=20 * 1024 * 1024),
            name="step",
        )(*operands)
        done = pl.pallas_call(
            put,
            out_shape=[jax.ShapeDtypeStruct(o.shape, o.dtype) for o in outs],
            in_specs=[pl.BlockSpec(memory_space=pl.ANY)] * 9,
            out_specs=[pl.BlockSpec(memory_space=pl.ANY)] * 9,
            scratch_shapes=[pltpu.SemaphoreType.DMA((9, LAYERS))],
            compiler_params=pltpu.CompilerParams(vmem_limit_bytes=1024 * 1024),
            name="put",
        )(*outs)
        whole = [o.reshape(a.shape) for o, a in zip(done[:3], arrays[3:6], strict=True)]
        return (*whole, *done[3:])

    all_of, part = P(None, None, None), P(None, "dp", None)
    return jax.shard_map(
        step,
        mesh=mesh,
        in_specs=(P(("rep", "dp"), None, None, None),) * 3 + (all_of,) * 3 + (part,) * 6,
        out_specs=(P("rep", None, None),) * 3 + (P("rep", "dp", None),) * 6,
        check_vma=False,
    )
```

time: 607 us -> 270 us (0.44)
  waiting for transfers between devices: 557 us -> 0 us
  Pallas kernels: 0 us -> 243 us
  between operations: 14.2 us -> 0.67 us
  other arithmetic: 11.6 us -> 0 us
    reduce_scatter x3 -> x0, waiting for transfers between devices: 369 us -> none  [step(): lax.psum_scatter(t[0], 'dp', scatter_dimension=1, tiled=True)]
    pallas_call x0 -> x2, Pallas kernels: none -> 243 us  [the longest x1 229 us: step(): pl.pallas_call(kernel, out_shape=[pltpu.VMEM((LAYERS, 2, 2, 2, 2, *s), BF...]
    all_gather x3 -> x0, waiting for transfers between devices: 185 us -> none  [step(): whole = [lax.all_gather(one[0], 'dp', axis=1, tiled=True) for one in new]]
    convert_element_type x3 -> x0, other arithmetic: 11.6 us -> none  [adamw(): return ((w - 0.02 * step).astype(jnp.bfloat16), m, v)]
    unnamed x19 -> x12, local copies, waits for them, and re-layouts: 24 us -> 26.1 us
  transfers between devices with their start and end apart: 6 -> 0, of which waited for: 6 -> 0; matrix products, arithmetic and copies ran while one was open for 2% -> 0% of each run, Pallas kernels for 0% -> 0%
where the time goes in v1:
time: 270 us
  Pallas kernels  243 us (90%)
  local copies, waits for them, and re-layouts  26.1 us (10%)
    pallas_call x1, Pallas kernels, step(): pl.pallas_call(kernel, out_shape=[pltpu.VMEM((LAYERS, 2, 2, 2, 2, *s), BF...  229 us
    unnamed x12, local copies, waits for them, and re-layouts  26.1 us
    pallas_call x1, Pallas kernels, step(): pl.pallas_call(put, out_shape=[jax.ShapeDtypeStruct(o.shape, o.dtype) for...  14 us

profile of v1, /device:TPU:0, one launch (start us, length us, event | category | flops | bytes accessed | tf_op | source)
XLA Modules:
  0.0 269.7 jit_solution(6832256513718065610)
XLA Ops:
  0.6 229.0 %step.1 = (bf16[2,2,2,2,2,64,2816]{6,5,4,3,2,1,0:T(8,128)(2,1)S(1)}, bf16[2,2,2,2,2,64,2816]{6,5,4,3,2,1,0:T(8,128)(2,1)S(1)}, bf16[2,2,2,2,2,176,1024]{6,5,4,3,...) custom-call(bf16[2,2,2,2,2,64,2816]{6,5,4,3,2,1,0:T(8,128)(2,1)} %bi, ...), custom_call_target="tpu_custom_call" | custom-call | tf_op jit(solution)/shard_map/step/pallas_call | solution.py:304
  229.6 0.0 copy-start
  229.6 4.4 %copy-done = bf16[2,2,2,2,2,64,2816]{6,5,4,3,2,1,0:T(8,128)(2,1)} copy-done((bf16[2,2,2,2,2,64,2816]{6,5,4,3,2,1,0:T(8,128)(2,1)}, bf16[2,2,2,2,2,64,2816]{6,5,4,3,2,1,0:T(8,128)(2,1)S(1)}, u32[]{:S(2)}) %copy-start) | copy-done | bytes 11534360
  234.0 0.0 copy-start.2
  234.1 4.4 %copy-done.2 = bf16[2,2,2,2,2,64,2816]{6,5,4,3,2,1,0:T(8,128)(2,1)} copy-done((bf16[2,2,2,2,2,64,2816]{6,5,4,3,2,1,0:T(8,128)(2,1)}, bf16[2,2,2,2,2,64,2816]{6,5,4,3,2,1,0:T(8,128)(2,1)S(1)}, u32[]{:S(2)}) %copy-start.2) | copy-done | bytes 11534360
  238.5 0.0 copy-start.4
  238.5 4.4 %copy-done.4 = bf16[2,2,2,2,2,176,1024]{6,5,4,3,2,1,0:T(8,128)(2,1)} copy-done((bf16[2,2,2,2,2,176,1024]{6,5,4,3,2,1,0:T(8,128)(2,1)}, bf16[2,2,2,2,2,176,1024]{6,5,4,3,2,1,0:T(8,128)(2,1)S(1)}, u32[]{:S(2)}) %copy-start.4) | copy-done | bytes 11534360
  242.9 0.0 copy-start.1
  242.9 4.3 %copy-done.1 = bf16[2,2,2,2,2,64,2816]{6,5,4,3,2,1,0:T(8,128)(2,1)S(1)} copy-done((bf16[2,2,2,2,2,64,2816]{6,5,4,3,2,1,0:T(8,128)(2,1)S(1)}, bf16[2,2,2,2,2,64,2816]{6,5,4,3,2,1,0:T(8,128)(2,1)}, u32[]{:S(2)}) %copy-start.1) | copy-done | bytes 11534360
  247.2 0.0 copy-start.3
  247.2 4.3 %copy-done.3 = bf16[2,2,2,2,2,64,2816]{6,5,4,3,2,1,0:T(8,128)(2,1)S(1)} copy-done((bf16[2,2,2,2,2,64,2816]{6,5,4,3,2,1,0:T(8,128)(2,1)S(1)}, bf16[2,2,2,2,2,64,2816]{6,5,4,3,2,1,0:T(8,128)(2,1)}, u32[]{:S(2)}) %copy-start.3) | copy-done | bytes 11534360
  251.5 0.0 copy-start.5
  251.5 4.3 %copy-done.5 = bf16[2,2,2,2,2,176,1024]{6,5,4,3,2,1,0:T(8,128)(2,1)S(1)} copy-done((bf16[2,2,2,2,2,176,1024]{6,5,4,3,2,1,0:T(8,128)(2,1)S(1)}, bf16[2,2,2,2,2,176,1024]{6,5,4,3,2,1,0:T(8,128)(2,1)}, u32[]{:S(2)}) %copy-start.5) | copy-done | bytes 11534360
  255.7 14.0 %put.1 = (bf16[2,2,2,2,2,64,2816]{6,5,4,3,2,1,0:T(8,128)(2,1)}, bf16[2,2,2,2,2,64,2816]{6,5,4,3,2,1,0:T(8,128)(2,1)}, bf16[2,2,2,2,2,176,1024]{6,5,4,3,2,1,0:T(8...) custom-call(bf16[2,2,2,2,2,64,2816]{6,5,4,3,2,1,0:T(8,128)(2,1)S(1)}, ...), custom_call_target="tpu_custom_call" | custom-call | tf_op jit(solution)/shard_map/put/pallas_call | solution.py:330
Async XLA Ops:
  229.6 4.4 %copy-start = (bf16[2,2,2,2,2,64,2816]{6,5,4,3,2,1,0:T(8,128)(2,1)}, bf16[2,2,2,2,2,64,2816]{6,5,4,3,2,1,0:T(8,128)(2,1)S(1)}, u32[]{:S(2)}) copy-start(bf16[2,2,2,2,2,64,2816]{6,5,4,3,2,1,0:T(8,128)(2,1)S(1)} %get-tuple-element.27.refs_0_) | copy-start | bytes 34603012
  234.0 4.4 %copy-start.2 = (bf16[2,2,2,2,2,64,2816]{6,5,4,3,2,1,0:T(8,128)(2,1)}, bf16[2,2,2,2,2,64,2816]{6,5,4,3,2,1,0:T(8,128)(2,1)S(1)}, u32[]{:S(2)}) copy-start(bf16[2,2,2,2,2,64,2816]{6,5,4,3,2,1,0:T(8,128)(2,1)S(1)} %get-tuple-element.28.refs_1_) | copy-start | bytes 34603012
  238.5 4.4 %copy-start.4 = (bf16[2,2,2,2,2,176,1024]{6,5,4,3,2,1,0:T(8,128)(2,1)}, bf16[2,2,2,2,2,176,1024]{6,5,4,3,2,1,0:T(8,128)(2,1)S(1)}, u32[]{:S(2)}) copy-start(bf16[2,2,2,2,2,176,1024]{6,5,4,3,2,1,0:T(8,128)(2,1)S(1)} %get-tuple-element.29.refs_2_) | copy-start | bytes 34603012
  242.9 4.3 %copy-start.1 = (bf16[2,2,2,2,2,64,2816]{6,5,4,3,2,1,0:T(8,128)(2,1)S(1)}, bf16[2,2,2,2,2,64,2816]{6,5,4,3,2,1,0:T(8,128)(2,1)}, u32[]{:S(2)}) copy-start(bf16[2,2,2,2,2,64,2816]{6,5,4,3,2,1,0:T(8,128)(2,1)} %copy-done) | copy-start | bytes 34603012
  247.2 4.3 %copy-start.3 = (bf16[2,2,2,2,2,64,2816]{6,5,4,3,2,1,0:T(8,128)(2,1)S(1)}, bf16[2,2,2,2,2,64,2816]{6,5,4,3,2,1,0:T(8,128)(2,1)}, u32[]{:S(2)}) copy-start(bf16[2,2,2,2,2,64,2816]{6,5,4,3,2,1,0:T(8,128)(2,1)} %copy-done.2) | copy-start | bytes 34603012
  251.5 4.3 %copy-start.5 = (bf16[2,2,2,2,2,176,1024]{6,5,4,3,2,1,0:T(8,128)(2,1)S(1)}, bf16[2,2,2,2,2,176,1024]{6,5,4,3,2,1,0:T(8,128)(2,1)}, u32[]{:S(2)}) copy-start(bf16[2,2,2,2,2,176,1024]{6,5,4,3,2,1,0:T(8,128)(2,1)} %copy-done.4) | copy-start | bytes 34603012

commit v2 on v1

--- a/solution.py
+++ b/solution.py
@@ -324,16 +324,17 @@
                 pltpu.SemaphoreType.REGULAR((3, 3)),
                 pltpu.SemaphoreType.REGULAR,
             ],
-            compiler_params=pltpu.CompilerParams(collective_id=0, has_side_effects=True, vmem_limit_bytes=20 * 1024 * 1024),
+            compiler_params=pltpu.CompilerParams(collective_id=0, has_side_effects=True, vmem_limit_bytes=17 * 1024 * 1024),
             name="step",
         )(*operands)
+        outs = [pltpu.with_memory_space_constraint(o, pltpu.VMEM) for o in outs]
         done = pl.pallas_call(
             put,
             out_shape=[jax.ShapeDtypeStruct(o.shape, o.dtype) for o in outs],
             in_specs=[pl.BlockSpec(memory_space=pl.ANY)] * 9,
             out_specs=[pl.BlockSpec(memory_space=pl.ANY)] * 9,
             scratch_shapes=[pltpu.SemaphoreType.DMA((9, LAYERS))],
-            compiler_params=pltpu.CompilerParams(vmem_limit_bytes=1024 * 1024),
+            compiler_params=pltpu.CompilerParams(vmem_limit_bytes=17 * 1024 * 1024),
             name="put",
         )(*outs)
         whole = [o.reshape(a.shape) for o, a in zip(done[:3], arrays[3:6], strict=True)]

time: 270 us -> 244 us (0.904)
  local copies, waits for them, and re-layouts: 26.1 us -> 0 us
    unnamed x12 -> x0, local copies, waits for them, and re-layouts: 26.1 us -> none
where the time goes in v2:
time: 244 us
  Pallas kernels  243 us (100%)
    pallas_call x1, Pallas kernels, step(): pl.pallas_call(kernel, out_shape=[pltpu.VMEM((LAYERS, 2, 2, 2, 2, *s), BF...  229 us
    pallas_call x1, Pallas kernels, step(): pl.pallas_call(put, out_shape=[jax.ShapeDtypeStruct(o.shape, o.dtype) for...  14 us

profile of v2, /device:TPU:0, one launch (start us, length us, event | category | flops | bytes accessed | tf_op | source)
XLA Modules:
  0.0 243.6 jit_solution(7588859314021346462)
XLA Ops:
  0.6 229.0 %step.1 = (bf16[2,2,2,2,2,64,2816]{6,5,4,3,2,1,0:T(8,128)(2,1)S(1)}, bf16[2,2,2,2,2,64,2816]{6,5,4,3,2,1,0:T(8,128)(2,1)S(1)}, bf16[2,2,2,2,2,176,1024]{6,5,4,3,...) custom-call(bf16[2,2,2,2,2,64,2816]{6,5,4,3,2,1,0:T(8,128)(2,1)} %bi, ...), custom_call_target="tpu_custom_call" | custom-call | tf_op jit(solution)/shard_map/step/pallas_call | solution.py:304
  229.6 14.0 %put.1 = (bf16[2,2,2,2,2,64,2816]{6,5,4,3,2,1,0:T(8,128)(2,1)}, bf16[2,2,2,2,2,64,2816]{6,5,4,3,2,1,0:T(8,128)(2,1)}, bf16[2,2,2,2,2,176,1024]{6,5,4,3,2,1,0:T(8...) custom-call(bf16[2,2,2,2,2,64,2816]{6,5,4,3,2,1,0:T(8,128)(2,1)S(1)}, ...), custom_call_target="tpu_custom_call" | custom-call | tf_op jit(solution)/shard_map/put/pallas_call | solution.py:331

commit v3 on v2

v3 whole, which is shorter than its diff:
```python
import jax
import jax.numpy as jnp
from jax import lax
from jax.experimental import pallas as pl
from jax.experimental.pallas import tpu as pltpu
from jax.sharding import PartitionSpec as P

BF16, F32 = jnp.bfloat16, jnp.float32
MESH = pl.DeviceIdType.MESH
LAYERS = 2
ORDERS = ((0, 1, 2), (1, 2, 0), (2, 0, 1))
STRIDES = (8, 4, 2)
SLAB = 16
PARTS = (16, 16, 48)


def adamw(w, m, v, g):
    m = 0.9 * m + 0.1 * g
    v = 0.95 * v + 0.05 * g * g
    step = m * lax.rsqrt(v + 1e-8) + 0.1 * w
    return (w - 0.02 * step).astype(BF16), m, v


class Weight:
    def __init__(self, order, where, core, **refs):
        self.order, self.core = order, core
        self.mine = [where[axis] for axis in order]
        self.__dict__.update(refs)

    def place(self, *stages):
        xyz = [None] * 3
        for axis, coordinate in zip(self.order, stages, strict=True):
            xyz[axis] = coordinate
        return tuple(xyz)

    def block(self, keep1, keep2, keep3):
        return self.place(*(1 - m + k * (2 * m - 1) for m, k in zip(self.mine, (keep1, keep2, keep3), strict=True)))


def kernel(*refs):
    g_refs, w_refs, m_refs, v_refs = (refs[i : i + 3] for i in (0, 3, 6, 9))
    all_refs, m_outs, v_outs = (refs[i : i + 3] for i in (12, 15, 18))
    firsts, seconds, thirds, olds = (refs[i : i + 3] for i in (21, 24, 27, 30))
    load_sem, pair_sem, s1_sem, s2_sem, s3_sem, a3_sem, a2_sem, a1_sem, a0_sem, send_sem, third_sem, free_sem, read_sem = refs[33:]

    me = lax.axis_index("dp")
    core = me % 2
    where = [(me // s) % 2 for s in STRIDES]
    partners = [me + s * (1 - 2 * b) for s, b in zip(STRIDES, where, strict=True)]
    pair = me + 1 - 2 * core

    weights = [
        Weight(
            ORDERS[i], where, core, i=i, part=PARTS[i], rows=olds[i].shape[1], g=g_refs[i], all=all_refs[i], m=m_outs[i], v=v_outs[i],
            first=firsts[i], second=seconds[i], third=thirds[i], old=olds[i],
            to=[partners[axis] for axis in ORDERS[i]],
        )
        for i in range(3)
    ]

    def remote(src, dst, send, recv, device):
        return pltpu.make_async_remote_copy(
            src_ref=src, dst_ref=dst, send_sem=send, recv_sem=recv, device_id={"dp": device}, device_id_type=MESH
        )

    def sent(w, n, like):
        remote(like, like, send_sem.at[w.i, n], a0_sem.at[w.i], pair).wait_send()

    def received(w, sem, like):
        remote(like, like, send_sem.at[w.i, 0], sem, pair).wait_recv()

    def unit(w, keep1, k):
        return (k % 2, *w.block(keep1, k // 4, (k // 2) % 2))

    def stage(w):
        return pltpu.make_async_copy(w.g.at[(slice(None), *w.block(0, 0, 0), 1 - core)], w.old, load_sem.at[w.i, 0])

    def load(w, keep2):
        at = (slice(None), *w.place(1 - w.mine[0], 1 - w.mine[1] + keep2 * (2 * w.mine[1] - 1), slice(None)), core)
        return pltpu.make_async_copy(w.g.at[at], w.all.at[at], load_sem.at[w.i, 1 + keep2])

    def load_rest(w):
        at = (slice(None), *w.place(w.mine[0], slice(None), slice(None)), core)
        return pltpu.make_async_copy(w.g.at[at], w.all.at[at], load_sem.at[w.i, 3])

    def load_m(w):
        return pltpu.make_async_copy(m_refs[w.i], w.m, load_sem.at[w.i, 4])

    def load_v(w):
        return pltpu.make_async_copy(v_refs[w.i], w.v, load_sem.at[w.i, 5])

    def load_w(w):
        return pltpu.make_async_copy(w_refs[w.i].at[(slice(None), *w.block(1, 1, 1), core)], w.old, load_sem.at[w.i, 6])

    def to_pair(w, keep1, k, recv):
        at = unit(w, keep1, k)
        return remote(w.g.at[(*at, 1 - core)], w.all.at[(*at, core)], send_sem.at[w.i, 0], pair_sem.at[w.i, recv], pair)

    def staged_to_pair(w, k, lo, n, recv):
        rows = pl.ds(lo, n)
        return remote(
            w.old.at[k, rows], w.all.at[(*unit(w, 0, k), core, rows)], send_sem.at[w.i, 0], pair_sem.at[w.i, recv], pair
        )

    def first(w, k, lo=0, n=None):
        rows = pl.ds(lo, w.rows if n is None else n)
        at = (*unit(w, 0, k), core, rows)
        return remote(w.all.at[at], w.first.at[k, rows], send_sem.at[w.i, 1], s1_sem.at[w.i, k // 2], w.to[0])

    def second(w, k):
        at = (k % 2, *w.block(1, 0, k // 2))
        return remote(w.all.at[(*at, core)], w.second.at[k], send_sem.at[w.i, 2], s2_sem.at[w.i, k // 2], w.to[1])

    def third(w, k):
        at = (k, *w.block(1, 1, 0))
        return remote(w.all.at[(*at, core)], w.third.at[k], third_sem.at[w.i, k], s3_sem.at[w.i, k], w.to[2])

    def tell(w, stage):
        pl.semaphore_signal(free_sem.at[w.i, stage], inc=1, device_id={"dp": w.to[stage]}, device_id_type=MESH)

    def told(w, stage):
        pl.semaphore_wait(free_sem.at[w.i, stage], 1)

    def gather3(w, k):
        at = (k, *w.block(1, 1, 1), core)
        return remote(w.all.at[at], w.all.at[at], send_sem.at[w.i, 3], a3_sem.at[w.i], w.to[2])

    def gather2(w, k):
        at = (k % 2, *w.block(1, 1, 1 - k // 2), core)
        return remote(w.all.at[at], w.all.at[at], send_sem.at[w.i, 4], a2_sem.at[w.i, k // 2], w.to[1])

    def came(w, keep1, k, lo, n):
        return (k % 2, *w.block(keep1, 1 - k // 4, 1 - (k // 2) % 2), core, pl.ds(lo, w.rows if n is None else n))

    def gather1(w, k, recv, lo=0, n=None):
        at = came(w, 1, k, lo, n)
        return remote(w.all.at[at], w.all.at[at], send_sem.at[w.i, 5], a1_sem.at[w.i, recv], w.to[0])

    def gather0(w, keep1, k, lo=0, n=None):
        at = came(w, keep1, k, lo, n)
        return remote(w.all.at[at], w.all.at[at], send_sem.at[w.i, 6], a0_sem.at[w.i], pair)

    def total(w, at, rows, *others):
        sum_ = w.all[(*at, core, rows, slice(None))].astype(F32) + w.all[(*at, 1 - core, rows, slice(None))].astype(F32)
        for other, k in others:
            sum_ = sum_ + other[k, rows, :].astype(F32)
        return sum_

    def slabs(lo, n, body):
        @pl.loop(0, n // SLAB)
        def _(r):
            body(pl.ds(pl.multiple_of(lo + r * SLAB, SLAB), SLAB))

    def add(w, at, *others, lo=0, n=None):
        def body(rows):
            w.all[(*at, core, rows, slice(None))] = total(w, at, rows, *others).astype(BF16)

        slabs(lo, w.rows if n is None else n, body)

    def each(lo, hi, body):
        @pl.loop(lo, hi)
        def _(k):
            body(k)

    for w in weights:
        stage(w).start()
    for keep2 in (0, 1):
        for w in weights:
            load(w, keep2).start()

    barrier = pltpu.get_barrier_semaphore()
    for device in (pair, *partners):
        pl.semaphore_signal(barrier, inc=1, device_id={"dp": device}, device_id_type=MESH)
    for w in weights:
        stage(w).wait()
    pl.semaphore_wait(barrier, 4)

    for w in weights:
        staged_to_pair(w, 0, 0, w.part, 0).start()
    for w in weights:
        staged_to_pair(w, 0, w.part, w.rows - w.part, 1).start()
    for w in weights:
        staged_to_pair(w, 1, 0, w.rows, 2).start()

    def start_pair(k):
        for w in weights:
            to_pair(w, 0, k, 3).start()

    each(2, 8, start_pair)

    def start_pair_rest(k):
        for w in weights:
            to_pair(w, 1, k, 4).start()

    each(0, 8, start_pair_rest)
    for w in weights:
        load_rest(w).start()

    for w in weights:
        load(w, 0).wait()
    for recv, k, begin, end in ((0, 0, 0, 1), (1, 0, 1, 2), (2, 1, 0, 2)):
        for w in weights:
            edges = (0, w.part, w.rows)
            lo, n = edges[begin], edges[end] - edges[begin]
            received(w, pair_sem.at[w.i, recv], w.old.at[0, pl.ds(0, n)])
            add(w, unit(w, 0, k), lo=lo, n=n)
            first(w, k, lo, n).start()
    for w in weights:
        load(w, 1).wait()
        received(w, pair_sem.at[w.i, 3], w.first.at[pl.ds(0, 6)])

    def stage1(k):
        for w in weights:
            add(w, unit(w, 0, k))
        for w in weights:
            first(w, k).start()

    each(2, 8, stage1)
    for w in weights:
        load_m(w).start()
        load_v(w).start()
        load_rest(w).wait()
        received(w, pair_sem.at[w.i, 4], w.first)
        sent(w, 0, w.all.at[:, :, :, :, core])
        load_w(w).start()

    def stage2(k):
        for w in weights:
            add(w, unit(w, 1, k), (w.first, k))
        for w in weights:
            second(w, k).start()

    for n in (0, 1):
        for w in weights:
            received(w, s1_sem.at[w.i, n], w.third)
        each(2 * n, 2 * n + 2, stage2)

    def stage3(k):
        for w in weights:
            add(w, unit(w, 1, 4 + k), (w.first, 4 + k), (w.second, k))
        for w in weights:
            third(w, k).start()

    for w in weights:
        received(w, s1_sem.at[w.i, 2], w.third)
        received(w, s2_sem.at[w.i, 0], w.third)
    each(0, 2, stage3)
    for w in weights:
        load_m(w).wait()
        load_v(w).wait()
        load_w(w).wait()
        sent(w, 1, w.first)
        tell(w, 0)
        received(w, s1_sem.at[w.i, 3], w.third)
        sent(w, 2, w.second)
        tell(w, 1)
        received(w, s2_sem.at[w.i, 1], w.third)

    def update(k):
        for w in weights:
            third(w, k).wait()
            tell(w, 2)
            at = (k, *w.block(1, 1, 1))

            def body(rows, w=w, at=at):
                g = total(w, at, rows, (w.first, 6 + k), (w.second, 2 + k), (w.third, k)).astype(BF16).astype(F32)
                new, m, v = adamw(w.old[k, rows, :].astype(F32), w.m[k, rows, :], w.v[k, rows, :], g)
                w.m[k, rows, :] = m
                w.v[k, rows, :] = v
                w.all[(*at, core, rows, slice(None))] = new

            slabs(0, w.rows, body)

        for w in weights:
            told(w, 2)
            gather3(w, k).start()

    each(0, 2, update)

    def own21(k):
        for w in weights:
            gather2(w, k).start()
        for w in weights:
            gather1(w, k, 0).start()

    for w in weights:
        told(w, 1)
        told(w, 0)
    each(0, 2, own21)

    pl.semaphore_signal(read_sem, inc=1, device_id={"dp": pair}, device_id_type=MESH)
    pl.semaphore_wait(read_sem, 1)

    def own0(k):
        for w in weights:
            gather0(w, 1, k).start()

    each(0, 2, own0)

    def back3(k):
        for w in weights:
            gather2(w, 2 + k).start()
        for w in weights:
            gather1(w, 2 + k, 1).start()
            gather0(w, 1, 2 + k).start()

    for w in weights:
        received(w, a3_sem.at[w.i], w.third)
    each(0, 2, back3)

    def back2(k):
        for w in weights:
            gather1(w, k, 2).start()
            gather0(w, 1, k).start()

    for w in weights:
        received(w, a2_sem.at[w.i, 0], w.third)
    each(4, 6, back2)
    for w in weights:
        received(w, a2_sem.at[w.i, 1], w.third)
        gather1(w, 6, 3).start()
    for w in weights:
        gather1(w, 7, 4, 0, w.rows - w.part).start()
    for w in weights:
        gather1(w, 7, 5, w.rows - w.part, w.part).start()
    for k in (6, 7):
        for w in weights:
            gather0(w, 1, k).start()

    def back1(k):
        for w in weights:
            gather0(w, 0, k).start()

    for n in (0, 1, 2):
        for w in weights:
            received(w, a1_sem.at[w.i, n], w.third)
        each(2 * n, 2 * n + 2, back1)
    for w in weights:
        received(w, a1_sem.at[w.i, 3], w.third.at[0])
        gather0(w, 0, 6).start()
    for w in weights:
        received(w, a1_sem.at[w.i, 4], w.third.at[0, pl.ds(0, w.rows - w.part)])
        gather0(w, 0, 7, 0, w.rows - w.part).start()
    for w in weights:
        received(w, a1_sem.at[w.i, 5], w.third.at[0, pl.ds(0, w.part)])
        gather0(w, 0, 7, w.rows - w.part, w.part).start()

    for w in weights:
        for n, like in ((3, w.third), (4, w.second), (5, w.first)):
            sent(w, n, like)
    for w in weights:
        received(w, a0_sem.at[w.i], w.all.at[:, :, :, :, 1 - core])
        sent(w, 6, w.all.at[:, :, :, :, core])


def put(*refs):
    sem = refs[-1]
    copies = [
        pltpu.make_async_copy(refs[i].at[k], refs[9 + i].at[k], sem.at[i, k]) for i in range(9) for k in range(LAYERS)
    ]
    for copy in copies:
        copy.start()
    for copy in copies:
        copy.wait()


def solution(mesh):
    def step(*arrays):
        shapes = [a.shape[1:] for a in arrays[6:9]]

        def cut(a, i):
            return a.reshape(LAYERS, 2, 2, 2, 2, *shapes[i])

        operands = [cut(a, n % 3) for n, a in enumerate(arrays[:6])] + list(arrays[6:])
        blocks = [(n, rows, columns) for n in (8, 4, 2, LAYERS) for rows, columns in shapes]
        outs = pl.pallas_call(
            kernel,
            out_shape=[pltpu.VMEM((LAYERS, 2, 2, 2, 2, *s), BF16) for s in shapes] + [pltpu.VMEM((LAYERS, *s), F32) for s in shapes] * 2,
            in_specs=[pl.BlockSpec(memory_space=pl.ANY)] * 12,
            out_specs=[pl.BlockSpec(memory_space=pltpu.VMEM)] * 9,
            scratch_shapes=[
                *(pltpu.VMEM(s, BF16) for s in blocks),
                *(pltpu.SemaphoreType.DMA((3, n)) for n in (7, 5, 4, 2, 2)),
                pltpu.SemaphoreType.DMA((3,)),
                *(pltpu.SemaphoreType.DMA((3, n)) for n in (2, 6)),
                pltpu.SemaphoreType.DMA((3,)),
                *(pltpu.SemaphoreType.DMA((3, n)) for n in (7, 2)),
                pltpu.SemaphoreType.REGULAR((3, 3)),
                pltpu.SemaphoreType.REGULAR,
            ],
            compiler_params=pltpu.CompilerParams(collective_id=0, has_side_effects=True, vmem_limit_bytes=17 * 1024 * 1024),
            name="step",
        )(*operands)
        outs = [pltpu.with_memory_space_constraint(o, pltpu.VMEM) for o in outs]
        done = pl.pallas_call(
            put,
            out_shape=[jax.ShapeDtypeStruct(o.shape, o.dtype) for o in outs],
            in_specs=[pl.BlockSpec(memory_space=pl.ANY)] * 9,
            out_specs=[pl.BlockSpec(memory_space=pl.ANY)] * 9,
            scratch_shapes=[pltpu.SemaphoreType.DMA((9, LAYERS))],
            compiler_params=pltpu.CompilerParams(vmem_limit_bytes=17 * 1024 * 1024),
            name="put",
        )(*outs)
        whole = [o.reshape(a.shape) for o, a in zip(done[:3], arrays[3:6], strict=True)]
        return (*whole, *done[3:])

    all_of, part = P(None, None, None), P(None, "dp", None)
    return jax.shard_map(
        step,
        mesh=mesh,
        in_specs=(P(("rep", "dp"), None, None, None),) * 3 + (all_of,) * 3 + (part,) * 6,
        out_specs=(P("rep", None, None),) * 3 + (P("rep", "dp", None),) * 6,
        check_vma=False,
    )
```

time: 244 us -> 241 us (0.988)
  Pallas kernels: 243 us -> 240 us
    pallas_call x1, Pallas kernels: 229 us -> 226 us  [step(): pl.pallas_call(kernel, out_shape=[pltpu.VMEM((LAYERS, 2, 2, 2, 2, *s), BF...]
where the time goes in v3:
time: 241 us; the launch traced here: 240 us
  Pallas kernels  240 us (100%)
    pallas_call x1, Pallas kernels, step(): pl.pallas_call(kernel, out_shape=[pltpu.VMEM((LAYERS, 2, 2, 2, 2, *s), BF...  226 us
    pallas_call x1, Pallas kernels, step(): pl.pallas_call(put, out_shape=[jax.ShapeDtypeStruct(o.shape, o.dtype) for...  14 us

profile of v3, /device:TPU:0, one launch (start us, length us, event | category | flops | bytes accessed | tf_op | source)
XLA Modules:
  0.0 240.4 jit_solution(3595755441537147848)
XLA Ops:
  0.6 225.8 %step.1 = (bf16[2,2,2,2,2,64,2816]{6,5,4,3,2,1,0:T(8,128)(2,1)S(1)}, bf16[2,2,2,2,2,64,2816]{6,5,4,3,2,1,0:T(8,128)(2,1)S(1)}, bf16[2,2,2,2,2,176,1024]{6,5,4,3,...) custom-call(bf16[2,2,2,2,2,64,2816]{6,5,4,3,2,1,0:T(8,128)(2,1)} %bi, ...), custom_call_target="tpu_custom_call" | custom-call | tf_op jit(solution)/shard_map/step/pallas_call | solution.py:376
  226.4 14.0 %put.1 = (bf16[2,2,2,2,2,64,2816]{6,5,4,3,2,1,0:T(8,128)(2,1)}, bf16[2,2,2,2,2,64,2816]{6,5,4,3,2,1,0:T(8,128)(2,1)}, bf16[2,2,2,2,2,176,1024]{6,5,4,3,2,1,0:T(8...) custom-call(bf16[2,2,2,2,2,64,2816]{6,5,4,3,2,1,0:T(8,128)(2,1)S(1)}, ...), custom_call_target="tpu_custom_call" | custom-call | tf_op jit(solution)/shard_map/put/pallas_call | solution.py:395

commit v4 on v3

--- a/solution.py
+++ b/solution.py
@@ -12,6 +12,7 @@
 STRIDES = (8, 4, 2)
 SLAB = 16
 PARTS = (16, 16, 48)
+PUT_FLOPS = 200_000_000
 
 
 def adamw(w, m, v, g):
@@ -39,9 +40,9 @@
 
 def kernel(*refs):
     g_refs, w_refs, m_refs, v_refs = (refs[i : i + 3] for i in (0, 3, 6, 9))
-    all_refs, m_outs, v_outs = (refs[i : i + 3] for i in (12, 15, 18))
-    firsts, seconds, thirds, olds = (refs[i : i + 3] for i in (21, 24, 27, 30))
-    load_sem, pair_sem, s1_sem, s2_sem, s3_sem, a3_sem, a2_sem, a1_sem, a0_sem, send_sem, third_sem, free_sem, read_sem = refs[33:]
+    all_refs, m_outs, v_outs, late_refs = (refs[i : i + 3] for i in (12, 15, 18, 21))
+    firsts, seconds, thirds, olds = (refs[i : i + 3] for i in (24, 27, 30, 33))
+    load_sem, pair_sem, s1_sem, s2_sem, s3_sem, a3_sem, a2_sem, a1_sem, a0_sem, send_sem, third_sem, free_sem, read_sem = refs[36:]
 
     me = lax.axis_index("dp")
     core = me % 2
@@ -52,7 +53,7 @@
     weights = [
         Weight(
             ORDERS[i], where, core, i=i, part=PARTS[i], rows=olds[i].shape[1], g=g_refs[i], all=all_refs[i], m=m_outs[i], v=v_outs[i],
-            first=firsts[i], second=seconds[i], third=thirds[i], old=olds[i],
+            first=firsts[i], second=seconds[i], third=thirds[i], old=olds[i], late=late_refs[i],
             to=[partners[axis] for axis in ORDERS[i]],
         )
         for i in range(3)
@@ -64,7 +65,7 @@
         )
 
     def sent(w, n, like):
-        remote(like, like, send_sem.at[w.i, n], a0_sem.at[w.i], pair).wait_send()
+        remote(like, like, send_sem.at[w.i, n], a0_sem.at[w.i, 0], pair).wait_send()
 
     def received(w, sem, like):
         remote(like, like, send_sem.at[w.i, 0], sem, pair).wait_recv()
@@ -138,7 +139,11 @@
 
     def gather0(w, keep1, k, lo=0, n=None):
         at = came(w, keep1, k, lo, n)
-        return remote(w.all.at[at], w.all.at[at], send_sem.at[w.i, 6], a0_sem.at[w.i], pair)
+        return remote(w.all.at[at], w.all.at[at], send_sem.at[w.i, 6 + keep1], a0_sem.at[w.i, keep1], pair)
+
+    def keep_late(w):
+        at = (slice(None), *w.block(1, 0, 0), core)
+        return pltpu.make_async_copy(w.all.at[at], w.late, load_sem.at[w.i, 0])
 
     def total(w, at, rows, *others):
         sum_ = w.all[(*at, core, rows, slice(None))].astype(F32) + w.all[(*at, 1 - core, rows, slice(None))].astype(F32)
@@ -310,47 +315,47 @@
 
     def back2(k):
         for w in weights:
-            gather1(w, k, 2).start()
             gather0(w, 1, k).start()
 
     for w in weights:
         received(w, a2_sem.at[w.i, 0], w.third)
+        gather1(w, 4, 2).start()
+    for w in weights:
+        gather1(w, 5, 3, 0, w.rows - w.part).start()
+    for w in weights:
+        gather1(w, 5, 4, w.rows - w.part, w.part).start()
     each(4, 6, back2)
     for w in weights:
         received(w, a2_sem.at[w.i, 1], w.third)
-        gather1(w, 6, 3).start()
-    for w in weights:
-        gather1(w, 7, 4, 0, w.rows - w.part).start()
-    for w in weights:
-        gather1(w, 7, 5, w.rows - w.part, w.part).start()
-    for k in (6, 7):
-        for w in weights:
-            gather0(w, 1, k).start()
+        keep_late(w).start()
+    each(6, 8, back2)
 
     def back1(k):
         for w in weights:
             gather0(w, 0, k).start()
 
-    for n in (0, 1, 2):
+    for n in (0, 1):
         for w in weights:
             received(w, a1_sem.at[w.i, n], w.third)
         each(2 * n, 2 * n + 2, back1)
     for w in weights:
-        received(w, a1_sem.at[w.i, 3], w.third.at[0])
-        gather0(w, 0, 6).start()
-    for w in weights:
-        received(w, a1_sem.at[w.i, 4], w.third.at[0, pl.ds(0, w.rows - w.part)])
-        gather0(w, 0, 7, 0, w.rows - w.part).start()
-    for w in weights:
-        received(w, a1_sem.at[w.i, 5], w.third.at[0, pl.ds(0, w.part)])
-        gather0(w, 0, 7, w.rows - w.part, w.part).start()
-
-    for w in weights:
-        for n, like in ((3, w.third), (4, w.second), (5, w.first)):
+        received(w, a1_sem.at[w.i, 2], w.third.at[0])
+        gather0(w, 0, 4).start()
+    for w in weights:
+        received(w, a1_sem.at[w.i, 3], w.third.at[0, pl.ds(0, w.rows - w.part)])
+        gather0(w, 0, 5, 0, w.rows - w.part).start()
+    for w in weights:
+        received(w, a1_sem.at[w.i, 4], w.third.at[0, pl.ds(0, w.part)])
+        gather0(w, 0, 5, w.rows - w.part, w.part).start()
+
+    for w in weights:
+        keep_late(w).wait()
+        for n, like in ((3, w.third), (4, w.second), (5, w.first.at[pl.ds(0, 6)]), (7, w.first)):
             sent(w, n, like)
-    for w in weights:
-        received(w, a0_sem.at[w.i], w.all.at[:, :, :, :, 1 - core])
-        sent(w, 6, w.all.at[:, :, :, :, core])
+        received(w, a0_sem.at[w.i, 1], w.first)
+    for w in weights:
+        received(w, a0_sem.at[w.i, 0], w.first.at[pl.ds(0, 6)])
+        sent(w, 6, w.first.at[pl.ds(0, 6)])
 
 
 def put(*refs):
@@ -364,6 +369,22 @@
         copy.wait()
 
 
+def patch(*refs):
+    lates, theirs, outs = (refs[i : i + 3] for i in (3, 6, 9))
+    sem = refs[12]
+    core = lax.axis_index("dp") % 2
+    where = [(lax.axis_index("dp") // s) % 2 for s in STRIDES]
+    copies = []
+    for i in range(3):
+        w = Weight(ORDERS[i], where, core)
+        for n, (src, side) in enumerate(((lates[i], core), (theirs[i], 1 - core))):
+            copies.append(pltpu.make_async_copy(src, outs[i].at[(slice(None), *w.block(0, 0, 0), side)], sem.at[i, n]))
+    for copy in copies:
+        copy.start()
+    for copy in copies:
+        copy.wait()
+
+
 def solution(mesh):
     def step(*arrays):
         shapes = [a.shape[1:] for a in arrays[6:9]]
@@ -375,32 +396,48 @@
         blocks = [(n, rows, columns) for n in (8, 4, 2, LAYERS) for rows, columns in shapes]
         outs = pl.pallas_call(
             kernel,
-            out_shape=[pltpu.VMEM((LAYERS, 2, 2, 2, 2, *s), BF16) for s in shapes] + [pltpu.VMEM((LAYERS, *s), F32) for s in shapes] * 2,
+            out_shape=[pltpu.VMEM((LAYERS, 2, 2, 2, 2, *s), BF16) for s in shapes] + [pltpu.VMEM((LAYERS, *s), F32) for s in shapes] * 2 + [jax.ShapeDtypeStruct((LAYERS, *s), BF16) for s in shapes],
             in_specs=[pl.BlockSpec(memory_space=pl.ANY)] * 12,
-            out_specs=[pl.BlockSpec(memory_space=pltpu.VMEM)] * 9,
+            out_specs=[pl.BlockSpec(memory_space=pltpu.VMEM)] * 9 + [pl.BlockSpec(memory_space=pl.ANY)] * 3,
             scratch_shapes=[
                 *(pltpu.VMEM(s, BF16) for s in blocks),
                 *(pltpu.SemaphoreType.DMA((3, n)) for n in (7, 5, 4, 2, 2)),
                 pltpu.SemaphoreType.DMA((3,)),
-                *(pltpu.SemaphoreType.DMA((3, n)) for n in (2, 6)),
-                pltpu.SemaphoreType.DMA((3,)),
-                *(pltpu.SemaphoreType.DMA((3, n)) for n in (7, 2)),
+                *(pltpu.SemaphoreType.DMA((3, n)) for n in (2, 5, 2, 8, 2)),
                 pltpu.SemaphoreType.REGULAR((3, 3)),
                 pltpu.SemaphoreType.REGULAR,
             ],
             compiler_params=pltpu.CompilerParams(collective_id=0, has_side_effects=True, vmem_limit_bytes=17 * 1024 * 1024),
             name="step",
         )(*operands)
-        outs = [pltpu.with_memory_space_constraint(o, pltpu.VMEM) for o in outs]
-        done = pl.pallas_call(
+        late = [lax.ppermute(o, "dp", [(d, d ^ STRIDES[order[0]]) for d in range(16)]) for o, order in zip(outs[9:], ORDERS, strict=True)]
+        outs = [pltpu.with_memory_space_constraint(o, pltpu.VMEM) for o in outs[:9]]
+        done = list(pl.pallas_call(
             put,
             out_shape=[jax.ShapeDtypeStruct(o.shape, o.dtype) for o in outs],
             in_specs=[pl.BlockSpec(memory_space=pl.ANY)] * 9,
             out_specs=[pl.BlockSpec(memory_space=pl.ANY)] * 9,
             scratch_shapes=[pltpu.SemaphoreType.DMA((9, LAYERS))],
             compiler_params=pltpu.CompilerParams(vmem_limit_bytes=17 * 1024 * 1024),
+            cost_estimate=pl.CostEstimate(flops=PUT_FLOPS, bytes_accessed=2 * 43_000_000, transcendentals=0),
             name="put",
-        )(*outs)
+        )(*outs))
+        for i in range(3):
+            late[i], done[3 + i] = lax.optimization_barrier((late[i], done[3 + i]))
+        theirs = [lax.ppermute(o, "dp", [(d, d ^ 1) for d in range(16)]) for o in late]
+        patched = pl.pallas_call(
+            patch,
+            out_shape=[jax.ShapeDtypeStruct(o.shape, o.dtype) for o in done[:3]],
+            in_specs=[pl.BlockSpec(memory_space=pl.ANY)] * 3 + [pl.BlockSpec(memory_space=pltpu.VMEM)] * 6,
+            out_specs=[pl.BlockSpec(memory_space=pl.ANY)] * 3,
+            input_output_aliases={0: 0, 1: 1, 2: 2},
+            scratch_shapes=[
+                pltpu.SemaphoreType.DMA((3, 2)),
+            ],
+            compiler_params=pltpu.CompilerParams(vmem_limit_bytes=17 * 1024 * 1024),
+            name="patch",
+        )(*done[:3], *(pltpu.with_memory_space_constraint(o, pltpu.VMEM) for o in (*late, *theirs)))
+        done = [*patched, *done[3:]]
         whole = [o.reshape(a.shape) for o, a in zip(done[:3], arrays[3:6], strict=True)]
         return (*whole, *done[3:])
 

time: 241 us -> 236 us (0.979)
  Pallas kernels: 240 us -> 226 us
  waiting for transfers between devices: 0 us -> 5.5 us
  starting transfers between devices: 0 us -> 3.57 us
    pallas_call x1, Pallas kernels: 226 us -> 210 us  [step(): pl.pallas_call(kernel, out_shape=[pltpu.VMEM((LAYERS, 2, 2, 2, 2, *s), BF...]
    ppermute x0 -> x6, waiting for transfers between devices: none -> 5.5 us  [the longest x3 3.31 us: step(): lax.ppermute(o, 'dp', [(d, d ^ STRIDES[order[0]]) for d in range(16)])]
    ppermute x0 -> x6, starting transfers between devices: none -> 3.57 us  [the longest x3 3.56 us: step(): lax.ppermute(o, 'dp', [(d, d ^ STRIDES[order[0]]) for d in range(16)])]
  transfers between devices with their start and end apart: 0 -> 6, of which waited for: 0 -> 5; matrix products, arithmetic and copies ran while one was open for 0% -> 0% of each run, Pallas kernels for 0% -> 6%
where the time goes in v4:
time: 236 us
  Pallas kernels  226 us (96%)
  waiting for transfers between devices  5.5 us (2%)
  starting transfers between devices  3.57 us (2%)
    pallas_call x1, Pallas kernels, step(): pl.pallas_call(kernel, out_shape=[pltpu.VMEM((LAYERS, 2, 2, 2, 2, *s), BF...  210 us
    pallas_call x1, Pallas kernels, step(): pl.pallas_call(put, out_shape=[jax.ShapeDtypeStruct(o.shape, o.dtype) for...  14 us
  transfers between devices with their start and end apart: 6, of which 5 were waited for; matrix products, arithmetic and copies ran while one was open for 0% of the time, Pallas kernels for 6%

profile of v4, /device:TPU:0, one launch (start us, length us, event | category | flops | bytes accessed | tf_op | source)
XLA Modules:
  0.0 236.1 jit_solution(4882143357237754524)
XLA Ops:
  0.6 210.3 %step.1 = (bf16[2,2,2,2,2,64,2816]{6,5,4,3,2,1,0:T(8,128)(2,1)S(1)}, bf16[2,2,2,2,2,64,2816]{6,5,4,3,2,1,0:T(8,128)(2,1)S(1)}, bf16[2,2,2,2,2,176,1024]{6,5,4,3,...) custom-call(bf16[2,2,2,2,2,64,2816]{6,5,4,3,2,1,0:T(8,128)(2,1)} %bi, ...), custom_call_target="tpu_custom_call" | custom-call | tf_op jit(solution)/shard_map/step/pallas_call | solution.py:397
  211.0 1.5 collective-permute-start
  212.5 1.5 collective-permute-start.1
  214.0 0.6 collective-permute-start.2
  214.6 14.0 %put.1 = (bf16[2,2,2,2,2,64,2816]{6,5,4,3,2,1,0:T(8,128)(2,1)}, bf16[2,2,2,2,2,64,2816]{6,5,4,3,2,1,0:T(8,128)(2,1)}, bf16[2,2,2,2,2,176,1024]{6,5,4,3,2,1,0:T(8...) custom-call(bf16[2,2,2,2,2,64,2816]{6,5,4,3,2,1,0:T(8,128)(2,1)S(1)}, ...), custom_call_target="tpu_custom_call" | custom-call | flops 200000000 | bytes 86000000 | tf_op jit(solution)/shard_map/put/pallas_call | solution.py:415
  228.5 0.9 collective-permute-done.refs_3_
  229.4 0.0 collective-permute-start.3
  229.4 1.2 collective-permute-done.1.refs_4_
  230.6 0.0 collective-permute-start.4
  230.6 1.2 collective-permute-done.2.refs_5_
  231.8 0.0 collective-permute-start.5
  231.9 0.0 collective-permute-done.3.refs_6_
  231.9 1.0 collective-permute-done.4.refs_7_
  232.8 1.2 collective-permute-done.5.refs_8_
  234.0 2.1 patch.1
Async XLA Ops:
  211.0 18.4 %collective-permute-start = (bf16[2,64,2816]{2,1,0:T(8,128)(2,1)}, bf16[2,64,2816]{2,1,0:T(8,128)(2,1)S(1)}, u32[]{:S(2)}, u32[]{:S(2)}) collective-permute-start(bf16[2,64,2816]{2,1,0:T(8,128)(2,1)} %get-tuple-element.51), channel_id=1, source_target_pairs={{0,8},{1,9},{2,10},{3,11},{4,12},{5,13},{6,14},{7,15},{8,0},{9,1},... | collective-permute-start | bytes 2162696 | tf_op jit(solution)/shard_map/ppermute | solution.py:413
  212.5 18.1 %collective-permute-start.1 = (bf16[2,64,2816]{2,1,0:T(8,128)(2,1)}, bf16[2,64,2816]{2,1,0:T(8,128)(2,1)S(1)}, u32[]{:S(2)}, u32[]{:S(2)}) collective-permute-start(bf16[2,64,2816]{2,1,0:T(8,128)(2,1)} %get-tuple-element.54), channel_id=1, source_target_pairs={{0,4},{1,5},{2,6},{3,7},{4,0},{5,1},{6,2},{7,3},{8,12},{9,13},{10,... | collective-permute-start | bytes 2162696 | tf_op jit(solution)/shard_map/ppermute | solution.py:413
  214.0 17.8 %collective-permute-start.2 = (bf16[2,176,1024]{2,1,0:T(8,128)(2,1)}, bf16[2,176,1024]{2,1,0:T(8,128)(2,1)S(1)}, u32[]{:S(2)}, u32[]{:S(2)}) collective-permute-start(bf16[2,176,1024]{2,1,0:T(8,128)(2,1)} %get-tuple-element.57), channel_id=1, source_target_pairs={{0,2},{1,3},{2,0},{3,1},{4,6},{5,7},{6,4},{7,5},{8,10},{9,11},{10,... | collective-permute-start | bytes 2162696 | tf_op jit(solution)/shard_map/ppermute | solution.py:413
  229.4 2.4 %collective-permute-start.3 = (bf16[2,64,2816]{2,1,0:T(8,128)(2,1)S(1)}, bf16[2,64,2816]{2,1,0:T(8,128)(2,1)S(1)}, u32[]{:S(2)}, u32[]{:S(2)}) collective-permute-start(bf16[2,64,2816]{2,1,0:T(8,128)(2,1)S(1)} %collective-permute-done.refs_3_), channel_id=1, source_target_pairs={{0,1},{1,0},{2,3},{3,2},{4,5},{5,4},{6,7},{7,6},{8,9},{9,8},{10,11... | collective-permute-start | bytes 2162696 | tf_op jit(solution)/shard_map/ppermute | solution.py:427
  230.6 2.2 collective-permute-start.4
  231.8 2.2 collective-permute-start.5

commit v5 on v4

v5 whole, which is shorter than its diff:
```python
import functools

import jax
import jax.numpy as jnp
from jax import lax
from jax.experimental import pallas as pl
from jax.experimental.pallas import tpu as pltpu
from jax.sharding import PartitionSpec as P

BF16, F32 = jnp.bfloat16, jnp.float32
MESH = pl.DeviceIdType.MESH
LAYERS = 2
ORDERS = ((0, 1, 2), (1, 2, 0), (2, 0, 1))
STRIDES = (8, 4, 2)
SLAB = 16
PARTS = (16, 16, 48)
PUT_FLOPS = 200_000_000


def adamw(w, m, v, g):
    m = 0.9 * m + 0.1 * g
    v = 0.95 * v + 0.05 * g * g
    step = m * lax.rsqrt(v + 1e-8) + 0.1 * w
    return (w - 0.02 * step).astype(BF16), m, v


class Weight:
    def __init__(self, order, where, core, **refs):
        self.order, self.core = order, core
        self.mine = [where[axis] for axis in order]
        self.__dict__.update(refs)

    def place(self, *stages):
        xyz = [None] * 3
        for axis, coordinate in zip(self.order, stages, strict=True):
            xyz[axis] = coordinate
        return tuple(xyz)

    def block(self, keep1, keep2, keep3):
        return self.place(*(1 - m + k * (2 * m - 1) for m, k in zip(self.mine, (keep1, keep2, keep3), strict=True)))


def kernel(*refs):
    g_refs, w_refs, m_refs, v_refs = (refs[i : i + 3] for i in (0, 3, 6, 9))
    all_refs, m_outs, v_outs, late_refs = (refs[i : i + 3] for i in (12, 15, 18, 21))
    firsts, seconds, thirds, olds = (refs[i : i + 3] for i in (24, 27, 30, 33))
    load_sem, pair_sem, rest_sem, s1_sem, s2_sem, s3_sem, a3_sem, a2_sem, a1_sem, last_sem, own_sem, a0_sem, all_send, send_sem, third_sem, free_sem, third_free, read_sem = refs[36:]

    me = lax.axis_index("dp")
    core = me % 2
    where = [(me // s) % 2 for s in STRIDES]
    partners = [me + s * (1 - 2 * b) for s, b in zip(STRIDES, where, strict=True)]
    pair = me + 1 - 2 * core

    weights = [
        Weight(
            ORDERS[i], where, core, i=i, part=PARTS[i], rows=olds[i].shape[1], g=g_refs[i], all=all_refs[i], m=m_outs[i], v=v_outs[i],
            first=firsts[i], second=seconds[i], third=thirds[i], old=olds[i], late=late_refs[i],
            to=[partners[axis] for axis in ORDERS[i]],
        )
        for i in range(3)
    ]

    def remote(src, dst, send, recv, device):
        return pltpu.make_async_remote_copy(
            src_ref=src, dst_ref=dst, send_sem=send, recv_sem=recv, device_id={"dp": device}, device_id_type=MESH
        )

    gate = weights[0]
    like = {
        2: gate.third,
        6: gate.first.at[pl.ds(0, 6)],
        8: gate.first,
        12: gate.all.at[:, :, :, :, 0, pl.ds(0, 48)],
        16: gate.all.at[:, :, :, :, 0],
        24: gate.all.at[:, :, :, :, :, pl.ds(0, 48)],
    }

    def sent(sem, ref):
        remote(ref, ref, sem, own_sem, pair).wait_send()

    def received(sem, ref):
        remote(ref, ref, own_sem, sem, pair).wait_recv()

    def loaded(n, ref):
        pltpu.make_async_copy(ref, ref, load_sem.at[n]).wait()

    def unit(w, keep1, k):
        return (k % 2, *w.block(keep1, k // 4, (k // 2) % 2))

    def stage(w):
        return pltpu.make_async_copy(w.g.at[(slice(None), *w.block(0, 0, 0), 1 - core)], w.old, load_sem.at[0])

    def load(w, keep2):
        at = (slice(None), *w.place(1 - w.mine[0], 1 - w.mine[1] + keep2 * (2 * w.mine[1] - 1), slice(None)), core)
        return pltpu.make_async_copy(w.g.at[at], w.all.at[at], load_sem.at[1 + keep2])

    def load_rest(w):
        at = (slice(None), *w.place(w.mine[0], slice(None), slice(None)), core)
        return pltpu.make_async_copy(w.g.at[at], w.all.at[at], load_sem.at[3])

    def load_m(w):
        return pltpu.make_async_copy(m_refs[w.i], w.m, load_sem.at[4])

    def load_v(w):
        return pltpu.make_async_copy(v_refs[w.i], w.v, load_sem.at[5])

    def load_w(w):
        return pltpu.make_async_copy(w_refs[w.i].at[(slice(None), *w.block(1, 1, 1), core)], w.old, load_sem.at[6])

    def to_pair(w, keep1, k):
        at, recv = unit(w, keep1, k), rest_sem if keep1 else pair_sem.at[w.i, 3]
        return remote(w.g.at[(*at, 1 - core)], w.all.at[(*at, core)], send_sem.at[w.i, 0], recv, pair)

    def staged_to_pair(w, k, lo, n, recv):
        rows = pl.ds(lo, n)
        return remote(
            w.old.at[k, rows], w.all.at[(*unit(w, 0, k), core, rows)], send_sem.at[w.i, 0], pair_sem.at[w.i, recv], pair
        )

    def first(w, k, lo=0, n=None):
        rows = pl.ds(lo, w.rows if n is None else n)
        at = (*unit(w, 0, k), core, rows)
        return remote(w.all.at[at], w.first.at[k, rows], all_send.at[0], s1_sem.at[k // 2], w.to[0])

    def second(w, k):
        at = (k % 2, *w.block(1, 0, k // 2))
        return remote(w.all.at[(*at, core)], w.second.at[k], all_send.at[1], s2_sem.at[k // 2], w.to[1])

    def third(w, k):
        at = (k, *w.block(1, 1, 0))
        return remote(w.all.at[(*at, core)], w.third.at[k], third_sem.at[w.i, k], s3_sem.at[w.i, k], w.to[2])

    def tell(n, stage):
        for w in weights:
            pl.semaphore_signal(free_sem.at[n], inc=1, device_id={"dp": w.to[stage]}, device_id_type=MESH)

    def told(n):
        pl.semaphore_wait(free_sem.at[n], 3)

    def gather3(w, k):
        at = (k, *w.block(1, 1, 1), core)
        return remote(w.all.at[at], w.all.at[at], all_send.at[2], a3_sem, w.to[2])

    def gather2(w, k):
        at = (k % 2, *w.block(1, 1, 1 - k // 2), core)
        return remote(w.all.at[at], w.all.at[at], all_send.at[3], a2_sem.at[k // 2], w.to[1])

    def came(w, keep1, k, lo, n):
        return (k % 2, *w.block(keep1, 1 - k // 4, 1 - (k // 2) % 2), core, pl.ds(lo, w.rows if n is None else n))

    def gather1(w, k, recv, lo=0, n=None):
        at = came(w, 1, k, lo, n)
        sem = a1_sem.at[recv] if recv < 2 else last_sem.at[w.i, recv - 2]
        return remote(w.all.at[at], w.all.at[at], send_sem.at[w.i, 1], sem, w.to[0])

    def gather0(w, keep1, k, lo=0, n=None):
        at = came(w, keep1, k, lo, n)
        send, recv = (all_send.at[4], own_sem) if keep1 else (send_sem.at[w.i, 2], a0_sem.at[w.i])
        return remote(w.all.at[at], w.all.at[at], send, recv, pair)

    def keep_late(w):
        at = (slice(None), *w.block(1, 0, 0), core)
        return pltpu.make_async_copy(w.all.at[at], w.late, load_sem.at[0])

    def total(w, at, rows, *others):
        sum_ = w.all[(*at, core, rows, slice(None))].astype(F32) + w.all[(*at, 1 - core, rows, slice(None))].astype(F32)
        for other, k in others:
            sum_ = sum_ + other[k, rows, :].astype(F32)
        return sum_

    def slabs(lo, n, body):
        @pl.loop(0, n // SLAB)
        def _(r):
            body(pl.ds(pl.multiple_of(lo + r * SLAB, SLAB), SLAB))

    def add(w, at, *others, lo=0, n=None):
        def body(rows):
            w.all[(*at, core, rows, slice(None))] = total(w, at, rows, *others).astype(BF16)

        slabs(lo, w.rows if n is None else n, body)

    def each(lo, hi, body):
        @pl.loop(lo, hi)
        def _(k):
            body(k)

    for w in weights:
        stage(w).start()
    for keep2 in (0, 1):
        for w in weights:
            load(w, keep2).start()

    barrier = pltpu.get_barrier_semaphore()
    for device in (pair, *partners):
        pl.semaphore_signal(barrier, inc=1, device_id={"dp": device}, device_id_type=MESH)
    loaded(0, like[6])
    pl.semaphore_wait(barrier, 4)

    for w in weights:
        staged_to_pair(w, 0, 0, w.part, 0).start()
    for w in weights:
        staged_to_pair(w, 0, w.part, w.rows - w.part, 1).start()
    for w in weights:
        staged_to_pair(w, 1, 0, w.rows, 2).start()

    def start_pair(k):
        for w in weights:
            to_pair(w, 0, k).start()

    each(2, 8, start_pair)

    def start_pair_rest(k):
        for w in weights:
            to_pair(w, 1, k).start()

    each(0, 8, start_pair_rest)
    for w in weights:
        load_rest(w).start()

    loaded(1, like[12])
    for recv, k, begin, end in ((0, 0, 0, 1), (1, 0, 1, 2), (2, 1, 0, 2)):
        for w in weights:
            edges = (0, w.part, w.rows)
            lo, n = edges[begin], edges[end] - edges[begin]
            received(pair_sem.at[w.i, recv], w.old.at[0, pl.ds(0, n)])
            add(w, unit(w, 0, k), lo=lo, n=n)
            first(w, k, lo, n).start()
    loaded(2, like[12])
    for w in weights:
        received(pair_sem.at[w.i, 3], like[6])

    def stage1(k):
        for w in weights:
            add(w, unit(w, 0, k))
        for w in weights:
            first(w, k).start()

    each(2, 8, stage1)
    for w in weights:
        load_m(w).start()
        load_v(w).start()
    loaded(3, like[24])
    received(rest_sem, like[24])
    for w in weights:
        sent(send_sem.at[w.i, 0], like[16])
        load_w(w).start()

    def stage2(k):
        for w in weights:
            add(w, unit(w, 1, k), (w.first, k))
        for w in weights:
            second(w, k).start()

    for n in (0, 1):
        received(s1_sem.at[n], like[6])
        each(2 * n, 2 * n + 2, stage2)

    def stage3(k):
        for w in weights:
            add(w, unit(w, 1, 4 + k), (w.first, 4 + k), (w.second, k))
        for w in weights:
            third(w, k).start()

    received(s1_sem.at[2], like[6])
    received(s2_sem.at[0], like[6])
    each(0, 2, stage3)
    loaded(4, like[12])
    loaded(5, like[12])
    loaded(6, like[6])
    sent(all_send.at[0], like[24])
    tell(0, 0)
    received(s1_sem.at[3], like[6])
    sent(all_send.at[1], like[12])
    tell(1, 1)
    received(s2_sem.at[1], like[6])

    def update(k):
        for w in weights:
            third(w, k).wait()
            pl.semaphore_signal(third_free.at[w.i], inc=1, device_id={"dp": w.to[2]}, device_id_type=MESH)
            at = (k, *w.block(1, 1, 1))

            def body(rows, w=w, at=at):
                g = total(w, at, rows, (w.first, 6 + k), (w.second, 2 + k), (w.third, k)).astype(BF16).astype(F32)
                new, m, v = adamw(w.old[k, rows, :].astype(F32), w.m[k, rows, :], w.v[k, rows, :], g)
                w.m[k, rows, :] = m
                w.v[k, rows, :] = v
                w.all[(*at, core, rows, slice(None))] = new

            slabs(0, w.rows, body)

        for w in weights:
            pl.semaphore_wait(third_free.at[w.i], 1)
            gather3(w, k).start()

    each(0, 2, update)

    def own21(k):
        for w in weights:
            gather2(w, k).start()
        for w in weights:
            gather1(w, k, 0).start()

    told(1)
    told(0)
    each(0, 2, own21)

    pl.semaphore_signal(read_sem, inc=1, device_id={"dp": pair}, device_id_type=MESH)
    pl.semaphore_wait(read_sem, 1)

    def own0(k):
        for w in weights:
            gather0(w, 1, k).start()

    each(0, 2, own0)

    def back3(k):
        for w in weights:
            gather2(w, 2 + k).start()
        for w in weights:
            gather1(w, 2 + k, 1).start()
            gather0(w, 1, 2 + k).start()

    received(a3_sem, like[6])
    each(0, 2, back3)

    def back2(k):
        for w in weights:
            gather0(w, 1, k).start()

    received(a2_sem.at[0], like[6])
    for w in weights:
        gather1(w, 4, 2).start()
    for w in weights:
        gather1(w, 5, 3, 0, w.rows - w.part).start()
    for w in weights:
        gather1(w, 5, 4, w.rows - w.part, w.part).start()
    each(4, 6, back2)
    received(a2_sem.at[1], like[6])
    for w in weights:
        keep_late(w).start()
    each(6, 8, back2)

    def back1(k):
        for w in weights:
            gather0(w, 0, k).start()

    for n in (0, 1):
        received(a1_sem.at[n], like[6])
        each(2 * n, 2 * n + 2, back1)
    for w in weights:
        received(last_sem.at[w.i, 0], w.third.at[0])
        gather0(w, 0, 4).start()
    for w in weights:
        received(last_sem.at[w.i, 1], w.third.at[0, pl.ds(0, w.rows - w.part)])
        gather0(w, 0, 5, 0, w.rows - w.part).start()
    for w in weights:
        received(last_sem.at[w.i, 2], w.third.at[0, pl.ds(0, w.part)])
        gather0(w, 0, 5, w.rows - w.part, w.part).start()

    loaded(0, like[6])
    for n, units in ((2, 6), (3, 12), (4, 24)):
        sent(all_send.at[n], like[units])
    received(own_sem, like[24])
    for w in weights:
        sent(send_sem.at[w.i, 1], like[6])
    for w in weights:
        received(a0_sem.at[w.i], like[6])
        sent(send_sem.at[w.i, 2], like[6])


def put(*refs):
    sem = refs[-1]
    copies = [
        pltpu.make_async_copy(refs[i].at[k], refs[9 + i].at[k], sem.at[i, k]) for i in range(9) for k in range(LAYERS)
    ]
    for copy in copies:
        copy.start()
    for copy in copies:
        copy.wait()


def patch(which, *refs):
    n = len({i for i, _ in which})
    blocks, outs, sem = refs[n : n + len(which)], refs[n + len(which) : -1], refs[-1]
    index = {i: j for j, i in enumerate(sorted({i for i, _ in which}))}
    core = lax.axis_index("dp") % 2
    where = [(lax.axis_index("dp") // s) % 2 for s in STRIDES]
    copies = []
    for j, ((i, paired), block) in enumerate(zip(which, blocks, strict=True)):
        at = (slice(None), *Weight(ORDERS[i], where, core).block(0, 0, 0), 1 - core if paired else core)
        copies.append(pltpu.make_async_copy(block, outs[index[i]].at[at], sem.at[j]))
    for copy in copies:
        copy.start()
    for copy in copies:
        copy.wait()


def solution(mesh):
    def step(*arrays):
        shapes = [a.shape[1:] for a in arrays[6:9]]

        def cut(a, i):
            return a.reshape(LAYERS, 2, 2, 2, 2, *shapes[i])

        operands = [cut(a, n % 3) for n, a in enumerate(arrays[:6])] + list(arrays[6:])
        blocks = [(n, rows, columns) for n in (8, 4, 2, LAYERS) for rows, columns in shapes]
        outs = pl.pallas_call(
            kernel,
            out_shape=[pltpu.VMEM((LAYERS, 2, 2, 2, 2, *s), BF16) for s in shapes] + [pltpu.VMEM((LAYERS, *s), F32) for s in shapes] * 2 + [jax.ShapeDtypeStruct((LAYERS, *s), BF16) for s in shapes],
            in_specs=[pl.BlockSpec(memory_space=pl.ANY)] * 12,
            out_specs=[pl.BlockSpec(memory_space=pltpu.VMEM)] * 9 + [pl.BlockSpec(memory_space=pl.ANY)] * 3,
            scratch_shapes=[
                *(pltpu.VMEM(s, BF16) for s in blocks),
                *(pltpu.SemaphoreType.DMA(n) for n in ((7,), (3, 4), (), (4,), (2,), (3, 2), (), (2,), (2,), (3, 3), (), (3,), (5,), (3, 3), (3, 2))),
                *(pltpu.SemaphoreType.REGULAR(n) for n in ((2,), (3,), ())),
            ],
            compiler_params=pltpu.CompilerParams(collective_id=0, has_side_effects=True, vmem_limit_bytes=17 * 1024 * 1024),
            name="step",
        )(*operands)
        late = [lax.ppermute(o, "dp", [(d, d ^ STRIDES[order[0]]) for d in range(16)]) for o, order in zip(outs[9:], ORDERS, strict=True)]
        outs = [pltpu.with_memory_space_constraint(o, pltpu.VMEM) for o in outs[:9]]
        done = list(pl.pallas_call(
            put,
            out_shape=[jax.ShapeDtypeStruct(o.shape, o.dtype) for o in outs],
            in_specs=[pl.BlockSpec(memory_space=pl.ANY)] * 9,
            out_specs=[pl.BlockSpec(memory_space=pl.ANY)] * 9,
            scratch_shapes=[pltpu.SemaphoreType.DMA((9, LAYERS))],
            compiler_params=pltpu.CompilerParams(vmem_limit_bytes=17 * 1024 * 1024),
            cost_estimate=pl.CostEstimate(flops=PUT_FLOPS, bytes_accessed=2 * 43_000_000, transcendentals=0),
            name="put",
        )(*outs))
        for i in range(3):
            late[i], done[3 + i] = lax.optimization_barrier((late[i], done[3 + i]))
        theirs = [lax.ppermute(o, "dp", [(d, d ^ 1) for d in range(16)]) for o in late]
        came = {(i, paired): (theirs if paired else late)[i] for i in range(3) for paired in (0, 1)}
        for name, which in (("patch0", ((0, 0), (1, 0), (2, 0), (0, 1))), ("patch1", ((1, 1), (2, 1)))):
            of = sorted({i for i, _ in which})
            patched = pl.pallas_call(
                functools.partial(patch, which),
                out_shape=[jax.ShapeDtypeStruct(done[i].shape, BF16) for i in of],
                in_specs=[pl.BlockSpec(memory_space=pl.ANY)] * len(of) + [pl.BlockSpec(memory_space=pltpu.VMEM)] * len(which),
                out_specs=[pl.BlockSpec(memory_space=pl.ANY)] * len(of),
                input_output_aliases={j: j for j in range(len(of))},
                scratch_shapes=[pltpu.SemaphoreType.DMA((len(which),))],
                compiler_params=pltpu.CompilerParams(vmem_limit_bytes=17 * 1024 * 1024),
                name=name,
            )(*(done[i] for i in of), *(pltpu.with_memory_space_constraint(came[one], pltpu.VMEM) for one in which))
            for i, one in zip(of, patched, strict=True):
                done[i] = one
        whole = [o.reshape(a.shape) for o, a in zip(done[:3], arrays[3:6], strict=True)]
        return (*whole, *done[3:])

    all_of, part = P(None, None, None), P(None, "dp", None)
    return jax.shard_map(
        step,
        mesh=mesh,
        in_specs=(P(("rep", "dp"), None, None, None),) * 3 + (all_of,) * 3 + (part,) * 6,
        out_specs=(P("rep", None, None),) * 3 + (P("rep", "dp", None),) * 6,
        check_vma=False,
    )
```

time: 236 us -> 235 us (level)
  transfers between devices with their start and end apart: 6 -> 6, of which waited for: 5 -> 4; matrix products, arithmetic and copies ran while one was open for 0% -> 0% of each run, Pallas kernels for 6% -> 7%
where the time goes in v5:
time: 235 us
  Pallas kernels  227 us (97%)
  waiting for transfers between devices  3.88 us (2%)
  starting transfers between devices  3.57 us (2%)
    pallas_call x1, Pallas kernels, step(): pl.pallas_call(kernel, out_shape=[pltpu.VMEM((LAYERS, 2, 2, 2, 2, *s), BF...  210 us
    pallas_call x1, Pallas kernels, step(): pl.pallas_call(put, out_shape=[jax.ShapeDtypeStruct(o.shape, o.dtype) for...  14 us
  transfers between devices with their start and end apart: 6, of which 4 were waited for; matrix products, arithmetic and copies ran while one was open for 0% of the time, Pallas kernels for 7%

profile of v5, /device:TPU:0, one launch (start us, length us, event | category | flops | bytes accessed | tf_op | source)
XLA Modules:
  0.0 234.7 jit_solution(11525758037807491415)
XLA Ops:
  0.6 209.9 %step.1 = (bf16[2,2,2,2,2,64,2816]{6,5,4,3,2,1,0:T(8,128)(2,1)S(1)}, bf16[2,2,2,2,2,64,2816]{6,5,4,3,2,1,0:T(8,128)(2,1)S(1)}, bf16[2,2,2,2,2,176,1024]{6,5,4,3,...) custom-call(bf16[2,2,2,2,2,64,2816]{6,5,4,3,2,1,0:T(8,128)(2,1)} %bi, ...), custom_call_target="tpu_custom_call" | custom-call | tf_op jit(solution)/shard_map/step/pallas_call | solution.py:409
  210.5 1.5 collective-permute-start
  212.0 1.5 collective-permute-start.1
  213.5 0.6 collective-permute-start.2
  214.1 14.0 %put.1 = (bf16[2,2,2,2,2,64,2816]{6,5,4,3,2,1,0:T(8,128)(2,1)}, bf16[2,2,2,2,2,64,2816]{6,5,4,3,2,1,0:T(8,128)(2,1)}, bf16[2,2,2,2,2,176,1024]{6,5,4,3,2,1,0:T(8...) custom-call(bf16[2,2,2,2,2,64,2816]{6,5,4,3,2,1,0:T(8,128)(2,1)S(1)}, ...), custom_call_target="tpu_custom_call" | custom-call | flops 200000000 | bytes 86000000 | tf_op jit(solution)/shard_map/put/pallas_call | solution.py:424
  228.0 0.9 collective-permute-done.refs_3_
  229.0 0.0 collective-permute-start.3
  229.0 1.2 collective-permute-done.1.refs_4_
  230.2 0.0 collective-permute-start.4
  230.2 1.2 collective-permute-done.2.refs_5_
  231.4 0.0 collective-permute-start.5
  231.4 0.0 collective-permute-done.3.refs_6_
  231.4 1.6 patch0.1
  233.0 0.0 collective-permute-done.4.refs_2_
  233.0 0.6 collective-permute-done.5.refs_3_
  233.6 1.1 patch1.1
Async XLA Ops:
  210.5 18.4 %collective-permute-start = (bf16[2,64,2816]{2,1,0:T(8,128)(2,1)}, bf16[2,64,2816]{2,1,0:T(8,128)(2,1)S(1)}, u32[]{:S(2)}, u32[]{:S(2)}) collective-permute-start(bf16[2,64,2816]{2,1,0:T(8,128)(2,1)} %get-tuple-element.53), channel_id=1, source_target_pairs={{0,8},{1,9},{2,10},{3,11},{4,12},{5,13},{6,14},{7,15},{8,0},{9,1},... | collective-permute-start | bytes 2162696 | tf_op jit(solution)/shard_map/ppermute | solution.py:422
  212.0 18.1 %collective-permute-start.1 = (bf16[2,64,2816]{2,1,0:T(8,128)(2,1)}, bf16[2,64,2816]{2,1,0:T(8,128)(2,1)S(1)}, u32[]{:S(2)}, u32[]{:S(2)}) collective-permute-start(bf16[2,64,2816]{2,1,0:T(8,128)(2,1)} %get-tuple-element.56), channel_id=1, source_target_pairs={{0,4},{1,5},{2,6},{3,7},{4,0},{5,1},{6,2},{7,3},{8,12},{9,13},{10,... | collective-permute-start | bytes 2162696 | tf_op jit(solution)/shard_map/ppermute | solution.py:422
  213.5 17.8 %collective-permute-start.2 = (bf16[2,176,1024]{2,1,0:T(8,128)(2,1)}, bf16[2,176,1024]{2,1,0:T(8,128)(2,1)S(1)}, u32[]{:S(2)}, u32[]{:S(2)}) collective-permute-start(bf16[2,176,1024]{2,1,0:T(8,128)(2,1)} %get-tuple-element.59), channel_id=1, source_target_pairs={{0,2},{1,3},{2,0},{3,1},{4,6},{5,7},{6,4},{7,5},{8,10},{9,11},{10,... | collective-permute-start | bytes 2162696 | tf_op jit(solution)/shard_map/ppermute | solution.py:422
  229.0 2.4 %collective-permute-start.3 = (bf16[2,64,2816]{2,1,0:T(8,128)(2,1)S(1)}, bf16[2,64,2816]{2,1,0:T(8,128)(2,1)S(1)}, u32[]{:S(2)}, u32[]{:S(2)}) collective-permute-start(bf16[2,64,2816]{2,1,0:T(8,128)(2,1)S(1)} %collective-permute-done.refs_3_), channel_id=1, source_target_pairs={{0,1},{1,0},{2,3},{3,2},{4,5},{5,4},{6,7},{7,6},{8,9},{9,8},{10,11... | collective-permute-start | bytes 2162696 | tf_op jit(solution)/shard_map/ppermute | solution.py:436
  230.2 2.8 %collective-permute-start.4 = (bf16[2,64,2816]{2,1,0:T(8,128)(2,1)S(1)}, bf16[2,64,2816]{2,1,0:T(8,128)(2,1)S(1)}, u32[]{:S(2)}, u32[]{:S(2)}) collective-permute-start(bf16[2,64,2816]{2,1,0:T(8,128)(2,1)S(1)} %collective-permute-done.1.refs_4_), channel_id=1, source_target_pairs={{0,1},{1,0},{2,3},{3,2},{4,5},{5,4},{6,7},{7,6},{8,9},{9,8},{10,11... | collective-permute-start | bytes 2162696 | tf_op jit(solution)/shard_map/ppermute | solution.py:436
  231.4 2.2 collective-permute-start.5
